TPU v7x, 32 devices: a whole 2x2x4 slice. The times are simulated.
32 devices in a mesh: q: 32 (over z, y, x, core).
Axes of the slice: x: 2, y: 2, z: 4, core: 2. Of those that a mesh axis runs over, the one named last changes fastest.
Arguments:
- state_in: float32 [2, 33554432], P(None, 'q')
- unitaries: float32 [2, 25, 2, 2], replicated
- cz_pairs: int32 [12, 2], replicated
Outputs:
- output 1: float32 [2, 33554432], P(None, 'q')
- output 2: float32 [25], replicated
All inputs are finite; a program needn't handle non-finite values.
Results may differ from a plain program's by a relative error of at most 0.001.
Values sent between devices are 32-bit elements.
A program may use at most 1 GiB of HBM per device.

v0:
```python
import jax
import jax.numpy as jnp
from jax import lax
from jax.sharding import PartitionSpec as P

LOW_BITS = 7
LANES = 2 ** LOW_BITS


def mix_pair(first, second, coef_a, coef_b):
    out_re = coef_a[0] * first[0] - coef_a[1] * first[1] + coef_b[0] * second[0] - coef_b[1] * second[1]
    out_im = coef_a[0] * first[1] + coef_a[1] * first[0] + coef_b[0] * second[1] + coef_b[1] * second[0]
    return jnp.stack([out_re, out_im])


def gate_wide(state, bit_pos, gate_mat):
    stride = state.shape[1] >> (bit_pos + 1)
    if stride >= 8 * LANES:
        view = state.reshape(2, 2 ** bit_pos, 2, stride // LANES, LANES)
        zero_half = view[:, :, 0]
        one_half = view[:, :, 1]
        new_zero = mix_pair(zero_half, one_half, gate_mat[:, 0, 0], gate_mat[:, 0, 1])
        new_one = mix_pair(zero_half, one_half, gate_mat[:, 1, 0], gate_mat[:, 1, 1])
        return jnp.stack([new_zero, new_one], axis=2).reshape(state.shape)
    view = state.reshape(2, 2 ** bit_pos, 2 * stride)
    zero_half = view[:, :, :stride]
    one_half = view[:, :, stride:]
    new_zero = mix_pair(zero_half, one_half, gate_mat[:, 0, 0], gate_mat[:, 0, 1])
    new_one = mix_pair(zero_half, one_half, gate_mat[:, 1, 0], gate_mat[:, 1, 1])
    return jnp.concatenate([new_zero, new_one], axis=2).reshape(state.shape)


def low_block(state, low_gates):
    block_re = jnp.ones((1, 1), jnp.float32)
    block_im = jnp.zeros((1, 1), jnp.float32)
    for bit_pos in range(LOW_BITS):
        tr_re = low_gates[0, bit_pos].T
        tr_im = low_gates[1, bit_pos].T
        next_re = block_re[:, None, :, None] * tr_re[None, :, None, :] - block_im[:, None, :, None] * tr_im[None, :, None, :]
        next_im = block_re[:, None, :, None] * tr_im[None, :, None, :] + block_im[:, None, :, None] * tr_re[None, :, None, :]
        block_size = 2 * block_re.shape[0]
        block_re = next_re.reshape(block_size, block_size)
        block_im = next_im.reshape(block_size, block_size)
    rows = state.reshape(2, -1, LANES)
    highest = lax.Precision.HIGHEST
    out_re = jnp.dot(rows[0], block_re, precision=highest, preferred_element_type=jnp.float32) - jnp.dot(rows[1], block_im, precision=highest, preferred_element_type=jnp.float32)
    out_im = jnp.dot(rows[0], block_im, precision=highest, preferred_element_type=jnp.float32) + jnp.dot(rows[1], block_re, precision=highest, preferred_element_type=jnp.float32)
    return jnp.stack([out_re, out_im]).reshape(state.shape)


def sign_grid(first_index, row_count, cz_pairs, num_qubits):
    row_index = lax.iota(jnp.int32, row_count)[:, None]
    col_index = lax.iota(jnp.int32, LANES)[None, :]
    flat_index = first_index + row_index * LANES + col_index
    parity = jnp.zeros_like(flat_index)
    for pair_pos in range(cz_pairs.shape[0]):
        shift_a = num_qubits - 1 - cz_pairs[pair_pos, 0]
        shift_b = num_qubits - 1 - cz_pairs[pair_pos, 1]
        parity = parity ^ ((flat_index >> shift_a) & (flat_index >> shift_b) & 1)
    return (1 - 2 * parity).astype(jnp.float32)


def bit_balance(density, row_bits):
    row_tot = jnp.sum(density, axis=1)
    col_tot = jnp.sum(density, axis=0)
    row_index = lax.iota(jnp.int32, density.shape[0])
    col_index = lax.iota(jnp.int32, LANES)
    row_part = [jnp.sum(row_tot * (1 - 2 * ((row_index >> (row_bits - 1 - bit_pos)) & 1)).astype(jnp.float32)) for bit_pos in range(row_bits)]
    col_part = [jnp.sum(col_tot * (1 - 2 * ((col_index >> (LOW_BITS - 1 - bit_pos)) & 1)).astype(jnp.float32)) for bit_pos in range(LOW_BITS)]
    return row_part + col_part


def solution(mesh):
    group_size = mesh.shape['q']
    top_bits = group_size.bit_length() - 1

    def local_layer(state_local, unitaries, cz_pairs):
        num_qubits = unitaries.shape[1]
        local_size = state_local.shape[1]
        row_count = local_size // LANES
        device = lax.axis_index('q')
        grid = state_local.reshape(2, row_count, LANES)
        for qubit_pos in range(top_bits):
            bit_shift = top_bits - 1 - qubit_pos
            flip_mask = 1 << bit_shift
            partner = lax.ppermute(grid, 'q', [(source, source ^ flip_mask) for source in range(group_size)])
            own_bit = (device >> bit_shift) & 1
            gate_mat = unitaries[:, qubit_pos]
            coef_self = jnp.where(own_bit == 1, gate_mat[:, 1, 1], gate_mat[:, 0, 0])
            coef_other = jnp.where(own_bit == 1, gate_mat[:, 1, 0], gate_mat[:, 0, 1])
            grid = mix_pair(grid, partner, coef_self, coef_other)
        state = grid.reshape(2, local_size)
        for qubit_pos in range(top_bits, num_qubits - LOW_BITS):
            state = gate_wide(state, qubit_pos - top_bits, unitaries[:, qubit_pos])
        state = low_block(state, unitaries[:, num_qubits - LOW_BITS:])
        grid = state.reshape(2, row_count, LANES) * sign_grid(device * local_size, row_count, cz_pairs, num_qubits)[None]
        density = grid[0] * grid[0] + grid[1] * grid[1]
        local_total = jnp.sum(density)
        top_part = [jnp.where(((device >> (top_bits - 1 - qubit_pos)) & 1) == 0, local_total, -local_total) for qubit_pos in range(top_bits)]
        low_part = bit_balance(density, num_qubits - top_bits - LOW_BITS)
        z_expect = lax.psum(jnp.stack(top_part + low_part), 'q') / (local_size * group_size)
        return grid.reshape(2, local_size), z_expect

    return jax.shard_map(local_layer, mesh=mesh, in_specs=(P(None, 'q'), P(), P()), out_specs=(P(None, 'q'), P()), check_vma=False)
```

profile of v0, /device:TPU:0, one launch (start us, length us, event | category | flops | bytes accessed | tf_op | source)
XLA Modules:
  0.0 1344.6 jit_solution(3201396640394599281)
XLA Ops:
  0.6 7.3 copy.279
  8.0 4.1 collective-permute-start
  13.0 12.4 multiply_subtract_fusion.6
  25.9 346.3 %collective-permute-done = f32[2,8192,128]{2,1,0:T(8,128)} collective-permute-done((f32[2,8192,128]{2,1,0:T(8,128)}, f32[2,8192,128]{2,1,0:T(8,128)}, u32[]{:S(2)}, u32[]{:S(2)}) %collective-permute-start) | collective-permute-done | bytes 8388640 | tf_op jit(solution)/shard_map/ppermute | solution.py:86
  372.2 5.3 multiply_subtract_fusion.5
  379.8 179.8 %collective-permute-done.1 = f32[2,8192,128]{2,1,0:T(8,128)S(1)} collective-permute-done((f32[2,8192,128]{2,1,0:T(8,128)S(1)}, f32[2,8192,128]{2,1,0:T(8,128)S(1)}, u32[]{:S(2)}, u32[]{:S(2)}) %collective-permute-start.1) | collective-permute-done | bytes 8388640 | tf_op jit(solution)/shard_map/ppermute | solution.py:86
  559.7 4.5 multiply_add_fusion.4
  564.2 4.3 pad_maximum_fusion.1
  572.5 178.2 %collective-permute-done.2 = f32[2,8192,128]{2,1,0:T(8,128)} collective-permute-done((f32[2,8192,128]{2,1,0:T(8,128)}, f32[2,8192,128]{2,1,0:T(8,128)}, u32[]{:S(2)}, u32[]{:S(2)}) %collective-permute-start.2) | collective-permute-done | bytes 8388640 | tf_op jit(solution)/shard_map/ppermute | solution.py:86
  750.6 9.3 multiply_subtract_fusion.3
  762.9 177.7 %collective-permute-done.3 = f32[2,8192,128]{2,1,0:T(8,128)S(1)} collective-permute-done((f32[2,8192,128]{2,1,0:T(8,128)S(1)}, f32[2,8192,128]{2,1,0:T(8,128)S(1)}, u32[]{:S(2)}, u32[]{:S(2)}) %collective-permute-start.3) | collective-permute-done | bytes 8388640 | tf_op jit(solution)/shard_map/ppermute | solution.py:86
  940.6 4.5 multiply_add_fusion.2
  945.1 4.3 pad_maximum_fusion.3
  955.2 3.9 multiply_subtract_fusion
  959.1 4.5 sub.1012
  963.7 4.7 add.1485
  990.3 10.0 subtract_convert_fusion
  1000.3 8.0 multiply_subtract_fusion.1
  1008.3 6.0 multiply_subtract_fusion.14
  1014.3 6.0 multiply_add_fusion.14
  1055.4 3.6 fusion.46
  1084.8 3.5 fusion.31
  1092.5 3.6 fusion.27
  1096.1 3.6 fusion.19
  1099.6 3.6 fusion.22
  1129.5 4.1 copy.238
  1133.6 9.3 reshape_reshape.44
  1142.9 7.6 multiply_subtract_fusion.12
  1150.4 3.5 multiply_subtract_fusion.11
  1154.0 3.7 maximum_maximum_fusion.1
  1157.7 9.3 reshape_reshape.45
  1167.1 7.4 multiply_subtract_fusion.10
  1174.5 3.5 multiply_subtract_fusion.9
  1178.0 4.1 maximum_maximum_fusion.2
  1182.1 9.3 reshape_reshape.46
  1191.4 7.4 multiply_subtract_fusion.8
  1202.9 3.9 fusion.77
  1206.8 4.7 squeeze.458
  1211.5 4.8 squeeze.473
  1216.3 5.6 fusion.103
  1221.9 3.6 fusion.104
  1225.5 3.6 convolution_subtract_fusion
  1229.2 3.6 convolution_add_fusion
  1241.8 12.5 stack.427
  1254.3 23.7 %add.1489 = s32[8192,1,128]{2,1,0:T(1,128)S(1)} broadcast(s32[8192]{0:T(1024)S(1)} %copy-done.17), dimensions={0} | broadcast | bytes 4227072 | tf_op jit(solution)/shard_map/add | solution.py:54
  1278.0 9.5 subtract_convert_fusion.1
  1287.5 42.7 %psum.7 = f32[25]{0:T(128)S(1)} all-reduce(f32[25]{0:T(128)S(1)} %stack.427), channel_id=1, replica_groups=mesh['q'=32] {'q'}, use_global_device_ids=true, to_apply=%region_23.24 | all-reduce | flops 25 | bytes 200 | tf_op jit(solution)/shard_map/psum | solution.py:101
  1330.7 13.6 %maximum_multiply_fusion = f32[2,1048576]{1,0:T(2,128)} fusion(f32[1,1048576]{1,0:T(1,128)} %bitcast.883, f32[1,1048576]{1,0:T(1,128)} %bitcast.881, f32[1048576]{0:T(1024)} %subtract_convert_fusion.1), kind=kLoop, calls=%fused_computation.20 | loop fusion | flops 4194304 | bytes 20971520 | tf_op jit(solution)/shard_map/mul | solution.py:96
  (162 shorter events, 123.9 us)
Async XLA Ops:
  0.6 11.4 copy-start.13
  8.0 364.2 %collective-permute-start = (f32[2,8192,128]{2,1,0:T(8,128)}, f32[2,8192,128]{2,1,0:T(8,128)}, u32[]{:S(2)}, u32[]{:S(2)}) collective-permute-start(f32[2,8192,128]{2,1,0:T(8,128)} %bitcast.855), channel_id=1, source_target_pairs={{0,16},{1,17},{2,18},{3,19},{4,20},{5,21},{6,22},{7,23},{8,24},{9,... | collective-permute-start | bytes 25165832 | tf_op jit(solution)/shard_map/ppermute | solution.py:86
  378.0 181.7 %collective-permute-start.1 = (f32[2,8192,128]{2,1,0:T(8,128)S(1)}, f32[2,8192,128]{2,1,0:T(8,128)S(1)}, u32[]{:S(2)}, u32[]{:S(2)}) collective-permute-start(f32[2,8192,128]{2,1,0:T(8,128)S(1)} %pad_maximum_fusion), channel_id=1, source_target_pairs={{0,8},{1,9},{2,10},{3,11},{4,12},{5,13},{6,14},{7,15},{8,0},{9,1},... | collective-permute-start | bytes 25165832 | tf_op jit(solution)/shard_map/ppermute | solution.py:86
  564.1 4.5 copy-start.10
  564.2 5.7 copy-start.11
  569.9 180.8 %collective-permute-start.2 = (f32[2,8192,128]{2,1,0:T(8,128)}, f32[2,8192,128]{2,1,0:T(8,128)}, u32[]{:S(2)}, u32[]{:S(2)}) collective-permute-start(f32[2,8192,128]{2,1,0:T(8,128)} %pad_maximum_fusion.1), channel_id=1, source_target_pairs={{0,4},{1,5},{2,6},{3,7},{4,0},{5,1},{6,2},{7,3},{8,12},{9,13},{10,... | collective-permute-start | bytes 25165832 | tf_op jit(solution)/shard_map/ppermute | solution.py:86
  760.5 180.1 %collective-permute-start.3 = (f32[2,8192,128]{2,1,0:T(8,128)S(1)}, f32[2,8192,128]{2,1,0:T(8,128)S(1)}, u32[]{:S(2)}, u32[]{:S(2)}) collective-permute-start(f32[2,8192,128]{2,1,0:T(8,128)S(1)} %pad_maximum_fusion.2), channel_id=1, source_target_pairs={{0,2},{1,3},{2,0},{3,1},{4,6},{5,7},{6,4},{7,5},{8,10},{9,11},{10,... | collective-permute-start | bytes 25165832 | tf_op jit(solution)/shard_map/ppermute | solution.py:86
  945.1 4.5 copy-start.7
  945.1 5.7 copy-start.9
  950.8 49.5 %collective-permute-start.4 = (f32[2,8192,128]{2,1,0:T(8,128)}, f32[2,8192,128]{2,1,0:T(8,128)}, u32[]{:S(2)}, u32[]{:S(2)}) collective-permute-start(f32[2,8192,128]{2,1,0:T(8,128)} %pad_maximum_fusion.3), channel_id=1, source_target_pairs={{0,1},{1,0},{2,3},{3,2},{4,5},{5,4},{6,7},{7,6},{8,9},{9,8},{10,11... | collective-permute-start | bytes 25165832 | tf_op jit(solution)/shard_map/ppermute | solution.py:86
  963.7 4.7 copy-start.18
  986.1 14.2 %copy-start.16 = (s32[8192]{0:T(1024)}, s32[8192]{0:T(1024)S(1)}, u32[]{:S(2)}) copy-start(s32[8192]{0:T(1024)S(1)} %multiply_add_fusion.18) | copy-start | bytes 98308
  990.3 10.1 copy-start.8
  1142.9 7.6 copy-start.1
  1167.1 7.4 copy-start.3
  1191.4 7.4 copy-start.2
  1211.5 4.8 copy-start.14
  1216.3 5.6 copy-start
  1216.3 5.6 copy-start.15
  1221.9 3.6 copy-start.6
  1229.2 3.7 copy-start.4
  1229.2 3.7 copy-start.12
  1232.8 1.9 copy-start.5
  1234.7 19.5 %copy-start.17 = (s32[8192]{0:T(1024)S(1)}, s32[8192]{0:T(1024)}, u32[]{:S(2)}) copy-start(s32[8192]{0:T(1024)} %copy-done.16) | copy-start | bytes 98308
where the time goes:
time: 1360 us; the launch traced here: 1340 us
  waiting for transfers between devices  882 us (65%)
  other arithmetic  250 us (18%)
  local copies, waits for them, and re-layouts  125 us (9%)
  blocking collectives  42.7 us (3%)
  between operations  20.7 us (2%)
  matrix products  16.4 us (1%)
    ppermute x5, waiting for transfers between devices, local_layer(): lax.ppermute(grid, 'q', [(source, source ^ flip_mask) for source in range...  882 us
    sub x29, other arithmetic, mix_pair(): coef_a[0] * first[0] - coef_a[1] * first[1] + coef_b[0] * second[0]  134 us
    psum x1, blocking collectives, local_layer(): lax.psum(jnp.stack(top_part + low_part), 'q') / (local_size * group_size)  42.7 us
    add x11, other arithmetic, mix_pair(): coef_a[0] * first[1] + coef_a[1] * first[0] + coef_b[0] * second[1]  40.8 us
    another operation x3, local copies, waits for them, and re-layouts, gate_wide(): view = state.reshape(2, 2 ** bit_pos, 2 * stride)  28 us
  transfers between devices with their start and end apart: 5, of which 4 were waited for; matrix products, arithmetic and copies ran while one was open for 4% of the time, Pallas kernels for 0%

commit v1 on v0

v1 whole, which is shorter than its diff:
```python
import jax
import jax.numpy as jnp
from jax import lax
from jax.experimental import pallas as pl
from jax.experimental.pallas import tpu as pltpu
from jax.sharding import PartitionSpec as P

MESH = pl.DeviceIdType.MESH
LANES = 128
ROWS = 8192
NG = 16
GR = ROWS // NG
NZ = 32
ZR = ROWS // NZ
BLK = 32
NQ = 25
HIGHEST = lax.Precision.HIGHEST


def loop(count, body, unroll=1):
    def step(i, carry):
        body(i)
        return carry
    lax.fori_loop(0, count, step, 0, unroll=unroll)


def cmac(terms):
    out_re = None
    out_im = None
    for (cr, ci), (xr, xi) in terms:
        re = cr * xr - ci * xi
        im = cr * xi + ci * xr
        out_re = re if out_re is None else out_re + re
        out_im = im if out_im is None else out_im + im
    return out_re, out_im


def cprod(a, b):
    return a[0] * b[0] - a[1] * b[1], a[0] * b[1] + a[1] * b[0]


def kernel(x_hbm, u_ref, cz_ref, o_hbm, z_ref,
           psi, abuf, bo, bf, xb, yb, cb, st, kl, ml, acc, tot, r1, r2,
           in_sem, out_sem, ps, ar, bor, bfr, fs, os_, xs, xr, ys, yr, cs, cr_, s1, g1, s2, g2):
    me = lax.axis_index('q')
    z = me // 8
    sub = me % 8
    b = z // 2
    inner = jnp.logical_or(z == 1, z == 2)
    outer = jnp.logical_not(inner)
    dev_out = sub + 24 * b
    dev_mid = sub + 8 * (3 - z)
    dev_in = sub + 8 * (1 + b)
    dev_mid = jnp.where(inner, dev_mid, dev_in)
    dev_out = jnp.where(inner, dev_out, dev_in)
    dev_x = me + 2 - 4 * ((me // 2) % 2)
    dev_y = me + 4 - 8 * ((me // 4) % 2)
    dev_c = me + 1 - 2 * (me % 2)

    def u(q, i, j):
        return u_ref[0, i, j, q], u_ref[1, i, j, q]

    def gate(q):
        return (u(q, 0, 0), u(q, 0, 1)), (u(q, 1, 0), u(q, 1, 1))

    def apply_pair(g, p0, p1):
        return cmac(((g[0][0], p0), (g[0][1], p1))), cmac(((g[1][0], p0), (g[1][1], p1)))

    def rows(start, size):
        return pl.ds(pl.multiple_of(start, 8), size)

    def load(ref, start, size):
        return ref[0, rows(start, size), :], ref[1, rows(start, size), :]

    def store(ref, start, size, val):
        ref[0, rows(start, size), :] = val[0]
        ref[1, rows(start, size), :] = val[1]

    def zslice(ref, k):
        return ref.at[:, rows(k * ZR, ZR), :]

    def gslice(ref, c):
        return ref.at[:, rows(c * GR, GR), :]

    def remote(src, dst, ss, rs, dev):
        return pltpu.make_async_remote_copy(src_ref=src, dst_ref=dst, send_sem=ss, recv_sem=rs,
                                            device_id=(dev,), device_id_type=MESH)

    def own_copy(k):
        return remote(zslice(psi, k), zslice(bo, k), ps.at[k], bor.at[k], dev_mid)

    def up_copy(k):
        return remote(zslice(psi, k), zslice(abuf, k), ps.at[k], ar.at[k], dev_in)

    def fwd_copy(k):
        return remote(zslice(abuf, k), zslice(bf, k), fs.at[k], bfr.at[k], dev_mid)

    def down_copy(k):
        return remote(zslice(abuf, k), zslice(bo, k), os_.at[k], bor.at[k], dev_out)

    def start_z(k):
        @pl.when(inner)
        def _():
            own_copy(k).start()

        @pl.when(outer)
        def _():
            up_copy(k).start()

    def forward(k):
        @pl.when(inner)
        def _():
            up_copy(k).wait_recv()
            fwd_copy(k).start()

    cd = u(0, b, b)
    co = u(0, b, 1 - b)
    w_own = (cprod(cd, u(1, 1 - b, 1 - b)), cprod(cd, u(1, 1 - b, b)),
             cprod(co, u(1, 1 - b, b)), cprod(co, u(1, 1 - b, 1 - b)))
    w_out = (cprod(cd, u(1, b, 1 - b)), cprod(cd, u(1, b, b)),
             cprod(co, u(1, b, b)), cprod(co, u(1, b, 1 - b)))

    def finish_z(k):
        @pl.when(inner)
        def _():
            own_copy(k).wait_send()
            fwd_copy(k).wait_send()
            own_copy(k).wait_recv()
            fwd_copy(k).wait_recv()

            def body(i):
                s = k * ZR + i * BLK
                vals = (load(psi, s, BLK), load(abuf, s, BLK), load(bo, s, BLK), load(bf, s, BLK))
                own = cmac(tuple(zip(w_own, vals)))
                out = cmac(tuple(zip(w_out, vals)))
                store(abuf, s, BLK, out)
                store(bo, s, BLK, own)
            loop(ZR // BLK, body)
            down_copy(k).start()

        @pl.when(outer)
        def _():
            up_copy(k).wait_send()
            down_copy(k).wait_recv()

    def xchg(state, c, stage):
        if stage == 0:
            return remote(gslice(state, c), gslice(xb, c), xs.at[c], xr.at[c], dev_x)
        if stage == 1:
            return remote(gslice(state, c), gslice(yb, c), ys.at[c], yr.at[c], dev_y)
        return remote(gslice(state, c), gslice(cb, c), cs.at[c], cr_.at[c], dev_c)

    bits = ((me // 2) % 2, (me // 4) % 2, me % 2)
    mix_coef = tuple((u(q, v, v), u(q, v, 1 - v)) for q, v in zip((3, 2, 4), bits))

    def mix(state, c, stage):
        cp = xchg(state, c, stage)
        cp.wait_send()
        cp.wait_recv()
        other = (xb, yb, cb)[stage]
        coef = mix_coef[stage]

        def body(i):
            s = c * GR + i * BLK
            store(state, s, BLK, cmac(((coef[0], load(state, s, BLK)), (coef[1], load(other, s, BLK)))))
        loop(GR // BLK, body, unroll=2)

    g9 = gate(9)
    g10 = gate(10)

    def local_gates(state, c):
        base = c * GR

        def rowgates(i):
            p = [load(state, base + j * 128 + i * 16, 16) for j in range(4)]
            p[0], p[2] = apply_pair(g9, p[0], p[2])
            p[1], p[3] = apply_pair(g9, p[1], p[3])
            p[0], p[1] = apply_pair(g10, p[0], p[1])
            p[2], p[3] = apply_pair(g10, p[2], p[3])
            for j in range(4):
                store(state, base + j * 128 + i * 16, 16, p[j])
        loop(8, rowgates)

        def mats(h):
            s = base + h * 256
            a = load(state, s, 128)
            d = load(state, s + 128, 128)
            packed = jnp.concatenate([jnp.concatenate([a[0], d[0]], axis=1),
                                      jnp.concatenate([a[1], d[1]], axis=1)], axis=0)
            m = jnp.dot(ml[...], packed, precision=HIGHEST, preferred_element_type=jnp.float32)
            packed = jnp.concatenate([jnp.concatenate([m[:128, :128], m[128:, :128]], axis=1),
                                      jnp.concatenate([m[:128, 128:], m[128:, 128:]], axis=1)], axis=0)
            m = jnp.dot(packed, kl[...], precision=HIGHEST, preferred_element_type=jnp.float32)
            store(state, s, 256, (m[:, :128], m[:, 128:]))
        loop(2, mats)

    g678 = (gate(6), gate(7), gate(8))

    def chunk_gates(state, first_row):
        def body(i):
            p = [load(state, first_row + j * GR + i * 8, 8) for j in range(8)]
            for g, step in zip(g678, (4, 2, 1)):
                for j in range(8):
                    if not j & step:
                        p[j], p[j + step] = apply_pair(g, p[j], p[j + step])
            for j in range(8):
                store(state, first_row + j * GR + i * 8, 8, p[j])
        loop(GR // 8, body)

    def in_copy(c, slot):
        return pltpu.make_async_copy(x_hbm.at[pl.ds(pl.multiple_of(c * 2 * GR, 8), 2 * GR), :],
                                     st.at[pl.ds(pl.multiple_of(slot * 2 * GR, 8), 2 * GR), :], in_sem.at[slot])

    g5 = gate(5)
    in_copy(0, 0).start()
    in_copy(8, 1).start()

    def phase0(c):
        slot = 2 * (c % 2)
        nxt = 2 - slot

        @pl.when(c < 7)
        def _():
            in_copy(c + 1, nxt).start()
            in_copy(c + 9, nxt + 1).start()
        in_copy(c, slot).wait()
        in_copy(c + 8, slot + 1).wait()

        def body(i):
            s0 = slot * 2 * GR + i * 2 * BLK
            s1_ = s0 + 2 * GR
            lo = st[pl.ds(s0, BLK, stride=2), :], st[pl.ds(s0 + 1, BLK, stride=2), :]
            hi = st[pl.ds(s1_, BLK, stride=2), :], st[pl.ds(s1_ + 1, BLK, stride=2), :]
            n0, n1 = apply_pair(g5, lo, hi)
            store(psi, c * GR + i * BLK, BLK, n0)
            store(psi, (c + 8) * GR + i * BLK, BLK, n1)
        loop(GR // BLK, body)
        start_z(2 * c)
        start_z(2 * c + 1)
    loop(8, phase0)

    row = lax.broadcasted_iota(jnp.int32, (128, 128), 0)
    col = lax.broadcasted_iota(jnp.int32, (128, 128), 1)

    def kron(first, out_idx, in_idx):
        val = None
        for j in range(7):
            g = gate(first + j)
            ob = ((out_idx >> (6 - j)) & 1) == 1
            ib = ((in_idx >> (6 - j)) & 1) == 1
            f = tuple(jnp.where(ob, jnp.where(ib, g[1][1][r], g[1][0][r]), jnp.where(ib, g[0][1][r], g[0][0][r]))
                      for r in range(2))
            val = f if val is None else cprod(val, f)
        return val
    km = kron(18, col, row)
    kl[0:128, 0:128] = km[0]
    kl[0:128, 128:256] = km[1]
    kl[128:256, 0:128] = -km[1]
    kl[128:256, 128:256] = km[0]
    mm = kron(11, row, col)
    ml[0:128, 0:128] = mm[0]
    ml[0:128, 128:256] = -mm[1]
    ml[128:256, 0:128] = mm[1]
    ml[128:256, 128:256] = mm[0]
    chunk_gates(psi, 8 * GR)

    def phase2(i):
        @pl.when(i < 8)
        def _():
            local_gates(psi, 8 + i)
            xchg(psi, 8 + i, 0).start()
            forward(2 * i)
            forward(2 * i + 1)

        @pl.when(jnp.logical_and(i >= 1, i < 9))
        def _():
            mix(psi, 7 + i, 0)
            xchg(psi, 7 + i, 1).start()

        @pl.when(jnp.logical_and(i >= 2, i < 10))
        def _():
            mix(psi, 6 + i, 1)
            xchg(psi, 6 + i, 2).start()

        @pl.when(i >= 3)
        def _():
            mix(psi, 5 + i, 2)
            start_z(2 * (5 + i))
            start_z(2 * (5 + i) + 1)
    loop(11, phase2)

    def phase3(i):
        @pl.when(i < 8)
        def _():
            forward(16 + 2 * i)
            forward(17 + 2 * i)
            finish_z(2 * i)
            finish_z(2 * i + 1)
            local_gates(bo, i)
            xchg(bo, i, 0).start()

        @pl.when(jnp.logical_and(i >= 1, i < 9))
        def _():
            mix(bo, i - 1, 0)
            xchg(bo, i - 1, 1).start()

        @pl.when(jnp.logical_and(i >= 2, i < 10))
        def _():
            mix(bo, i - 2, 1)
            xchg(bo, i - 2, 2).start()

        @pl.when(i >= 3)
        def _():
            mix(bo, i - 3, 2)
    loop(11, phase3)

    chunk_gates(bo, 0)
    acc[...] = jnp.zeros_like(acc)
    flat = lax.broadcasted_iota(jnp.int32, (BLK, LANES), 0) * LANES + lax.broadcasted_iota(jnp.int32, (BLK, LANES), 1)
    shifts = [(NQ - 1 - cz_ref[0, p], NQ - 1 - cz_ref[1, p]) for p in range(12)]

    def out_copy(k):
        slot = k % 4
        return pltpu.make_async_copy(st.at[pl.ds(pl.multiple_of(slot * 2 * ZR, 8), 2 * ZR), :],
                                     o_hbm.at[pl.ds(pl.multiple_of(k * 2 * ZR, 8), 2 * ZR), :], out_sem.at[slot])

    def emit(k, wait):
        if wait:
            out_copy(k - 4).wait()
        slot = k % 4
        tot[k] = jnp.zeros((8, LANES), jnp.float32)

        def body(i):
            re, im = load(bo, k * ZR + i * BLK, BLK)
            idx = flat + (me * (ROWS * LANES) + (k * ZR + i * BLK) * LANES)
            par = None
            for sa, sb in shifts:
                t = lax.shift_right_logical(idx, sa) & lax.shift_right_logical(idx, sb)
                par = t if par is None else par ^ t
            sign = (1 - 2 * (par & 1)).astype(jnp.float32)
            d = re * re + im * im
            acc[rows(i * BLK, BLK), :] += d
            t8 = d[0:8]
            for j in range(1, BLK // 8):
                t8 = t8 + d[8 * j:8 * j + 8]
            tot[k] += t8
            s = slot * 2 * ZR + i * 2 * BLK
            st[pl.ds(s, BLK, stride=2), :] = re * sign
            st[pl.ds(s + 1, BLK, stride=2), :] = im * sign
        loop(ZR // BLK, body)
        out_copy(k).start()
    loop(4, lambda k: emit(k, False))
    loop(12, lambda k: emit(k + 4, True))

    def phase5(j):
        finish_z(16 + j)
        emit(16 + j, True)
    loop(16, phase5)
    loop(4, lambda k: out_copy(28 + k).wait())

    @pl.when(inner)
    def _():
        loop(NZ, lambda k: down_copy(k).wait_send())

    t8 = tot[0]
    for k in range(1, NZ):
        t8 = t8 + tot[k]

    def signed(count, get, bit):
        val = None
        for v in range(count):
            t = get(v)
            neg = (v >> bit) & 1
            if val is None:
                val = t
            else:
                val = val - t if neg else val + t
        return val
    sl = lax.broadcasted_iota(jnp.int32, (8, LANES), 0)
    ln = lax.broadcasted_iota(jnp.int32, (8, LANES), 1)
    vecs = []
    for q in range(5):
        sgn = (1 - 2 * ((me >> (4 - q)) & 1)).astype(jnp.float32)
        vecs.append(t8 * sgn)
    for q in range(5, 10):
        vecs.append(signed(NZ, lambda v: tot[v], 9 - q))
    for q in range(10, 15):
        vecs.append(signed(ZR // 8, lambda v: acc[8 * v:8 * v + 8, :], 14 - q))
    for q in range(15, 18):
        vecs.append(t8 * (1 - 2 * ((sl >> (17 - q)) & 1)).astype(jnp.float32))
    for q in range(18, 25):
        vecs.append(t8 * (1 - 2 * ((ln >> (24 - q)) & 1)).astype(jnp.float32))
    parts = [jnp.sum(v, axis=0, keepdims=True) for v in vecs]
    parts += [jnp.zeros((1, LANES), jnp.float32)] * (32 - NQ)
    r1[pl.ds(sub, 1)] = jnp.concatenate(parts, axis=0)[None]

    def peer1(r):
        p = sub ^ r
        return p, z * 8 + p

    for r in range(1, 8):
        p, dev = peer1(r)
        remote(r1.at[sub], r1.at[sub], s1.at[p], g1.at[sub], dev).start()
    for r in range(1, 8):
        p, dev = peer1(r)
        remote(r1.at[sub], r1.at[p], s1.at[p], g1.at[p], dev).wait_recv()
    val = r1[0]
    for p in range(1, 8):
        val = val + r1[p]
    r2[pl.ds(z, 1)] = val[None]
    for r in range(1, 4):
        p = z ^ r
        remote(r2.at[z], r2.at[z], s2.at[p], g2.at[z], p * 8 + sub).start()
    for r in range(1, 4):
        p = z ^ r
        remote(r2.at[z], r2.at[p], s2.at[p], g2.at[p], p * 8 + sub).wait_recv()
    val = ((r2[0] + r2[1]) + r2[2]) + r2[3]
    for r in range(1, 8):
        p, dev = peer1(r)
        remote(r1.at[sub], r1.at[sub], s1.at[p], g1.at[sub], dev).wait_send()
    for r in range(1, 4):
        p = z ^ r
        remote(r2.at[z], r2.at[z], s2.at[p], g2.at[z], p * 8 + sub).wait_send()
    wide = jnp.concatenate([val, jnp.zeros((LANES - 32, LANES), jnp.float32)], axis=0)
    zrow = jnp.sum(wide.T, axis=0, keepdims=True) * (1.0 / (ROWS * LANES * 32))
    z_ref[...] = zrow[:, :NQ]


def solution(mesh):
    dma = pltpu.SemaphoreType.DMA
    big = pltpu.VMEM((2, ROWS, LANES), jnp.float32)

    def local_layer(state_local, unitaries, cz_pairs):
        x = state_local.reshape(2, ROWS, LANES).transpose(1, 0, 2).reshape(2 * ROWS, LANES)
        gates = unitaries.transpose(0, 2, 3, 1)
        out, z_exp = pl.pallas_call(
            kernel,
            name="gate_layer",
            out_shape=(jax.ShapeDtypeStruct((2 * ROWS, LANES), jnp.float32),
                       jax.ShapeDtypeStruct((1, NQ), jnp.float32)),
            in_specs=[pl.BlockSpec(memory_space=pl.ANY),
                      pl.BlockSpec(memory_space=pltpu.SMEM),
                      pl.BlockSpec(memory_space=pltpu.SMEM)],
            out_specs=(pl.BlockSpec(memory_space=pl.ANY), pl.BlockSpec(memory_space=pltpu.VMEM)),
            scratch_shapes=[big] * 7 + [
                pltpu.VMEM((4 * 2 * GR, LANES), jnp.float32),
                pltpu.VMEM((256, 256), jnp.float32),
                pltpu.VMEM((256, 256), jnp.float32),
                pltpu.VMEM((ZR, LANES), jnp.float32),
                pltpu.VMEM((NZ, 8, LANES), jnp.float32),
                pltpu.VMEM((8, 32, LANES), jnp.float32),
                pltpu.VMEM((4, 32, LANES), jnp.float32),
                dma((4,)), dma((4,)),
                dma((NZ,)), dma((NZ,)), dma((NZ,)), dma((NZ,)), dma((NZ,)), dma((NZ,)),
                dma((NG,)), dma((NG,)), dma((NG,)), dma((NG,)), dma((NG,)), dma((NG,)),
                dma((8,)), dma((8,)), dma((4,)), dma((4,))],
            compiler_params=pltpu.CompilerParams(has_side_effects=True, vmem_limit_bytes=66_000_000),
        )(x, gates, cz_pairs.transpose(1, 0))
        out = out.reshape(ROWS, 2, LANES).transpose(1, 0, 2).reshape(2, ROWS * LANES)
        return out, z_exp.reshape(NQ)

    return jax.shard_map(local_layer, mesh=mesh, in_specs=(P(None, 'q'), P(), P()),
                         out_specs=(P(None, 'q'), P()), check_vma=False)
```

time: 1360 us -> 401 us (0.29); the launches traced: 1340 us -> 401 us
  waiting for transfers between devices: 882 us -> 0 us
  Pallas kernels: 0 us -> 392 us
  other arithmetic: 250 us -> 0 us
  local copies, waits for them, and re-layouts: 125 us -> 7.82 us
  blocking collectives: 42.7 us -> 0 us
  between operations: 20.7 us -> 0.65 us
  matrix products: 16.4 us -> 0 us
    ppermute x5 -> x0, waiting for transfers between devices: 882 us -> none  [local_layer(): lax.ppermute(grid, 'q', [(source, source ^ flip_mask) for source in range...]
    pallas_call x0 -> x1, Pallas kernels: none -> 392 us  [local_layer(): pl.pallas_call(kernel, name='gate_layer', out_shape=(jax.ShapeDtypeStruct...]
    sub x36 -> x0, other arithmetic: 139 us -> none  [the longest x29 134 us: mix_pair(): coef_a[0] * first[0] - coef_a[1] * first[1] + coef_b[0] * second[0]]
    another operation x12 -> x0, local copies, waits for them, and re-layouts: 52.7 us -> none  [the longest x3 28 us: gate_wide(): view = state.reshape(2, 2 ** bit_pos, 2 * stride)]
    psum x1 -> x0, blocking collectives: 42.7 us -> none  [local_layer(): lax.psum(jnp.stack(top_part + low_part), 'q') / (local_size * group_size)]
    add x12 -> x0, other arithmetic: 40.9 us -> none  [the longest x11 40.8 us: mix_pair(): coef_a[0] * first[1] + coef_a[1] * first[0] + coef_b[0] * second[1]]
    add x8 -> x0, local copies, waits for them, and re-layouts: 29.5 us -> none  [the longest x1 23.7 us: sign_grid(): flat_index = first_index + row_index * LANES + col_index]
    another operation x32 -> x0, other arithmetic: 23.7 us -> none  [the longest x28 14.1 us: gate_wide(): return jnp.stack([new_zero, new_one], axis=2).reshape(state.shape)]
  transfers between devices with their start and end apart: 5 -> 0, of which waited for: 4 -> 0; matrix products, arithmetic and copies ran while one was open for 4% -> 0% of each run, Pallas kernels for 0% -> 0%
where the time goes in v1:
time: 401 us
  Pallas kernels  392 us (98%)
  local copies, waits for them, and re-layouts  7.82 us (2%)
    pallas_call x1, Pallas kernels, local_layer(): pl.pallas_call(kernel, name='gate_layer', out_shape=(jax.ShapeDtypeStruct...  392 us

profile of v1, /device:TPU:0, one launch (start us, length us, event | category | flops | bytes accessed | tf_op | source)
XLA Modules:
  0.0 400.8 jit_solution(17769680001633833454)
XLA Ops:
  0.6 392.3 %gate_layer.1 = (f32[16384,128]{1,0:T(8,128)}, f32[1,25]{1,0:T(1,128)}) custom-call(f32[16384,128]{1,0:T(8,128)} %bitcast.13, f32[2,2,2,25]{3,2,1,0:T(2,128)} %bitcast.15, s32[2,12]{1,0:T(2,128)} %bitcast.16), custom_call_target="tpu_custom_call" | custom-call | tf_op jit(solution)/shard_map/gate_layer/pallas_call | solution.py:436
  393.0 0.0 copy-start
  393.0 7.3 %copy.9 = f32[2,1048576]{1,0:T(2,128)} copy(f32[2,1048576]{1,0:T(2,128)} %bitcast.14) | data formatting | bytes 16777216
  400.3 0.0 copy-done
  400.3 0.5 copy.10
Async XLA Ops:
  393.0 7.3 %copy-start = (f32[1,25]{1,0:T(1,128)S(1)}, f32[1,25]{1,0:T(1,128)}, u32[]{:S(2)}) copy-start(f32[1,25]{1,0:T(1,128)} %get-tuple-element.5) | copy-start | bytes 304

commit v2 on v1

v2 whole, which is shorter than its diff:
```python
import jax
import jax.numpy as jnp
from jax import lax
from jax.experimental import pallas as pl
from jax.experimental.pallas import tpu as pltpu
from jax.sharding import PartitionSpec as P

MESH = pl.DeviceIdType.MESH
LANES = 128
ROWS = 8192
NG = 16
GR = ROWS // NG
NF = 8
NS = 32
SR = 128
HALF = ROWS // 2
BLK = 32
NQ = 25
HIGHEST = lax.Precision.HIGHEST
VMEM_LIMIT = 50 * 2 ** 20


def loop(count, body, unroll=1):
    def step(i, carry):
        body(i)
        return carry
    lax.fori_loop(0, count, step, 0, unroll=unroll)


def cmac(terms):
    out_re = None
    out_im = None
    for (cr, ci), (xr, xi) in terms:
        re = cr * xr - ci * xi
        im = cr * xi + ci * xr
        out_re = re if out_re is None else out_re + re
        out_im = im if out_im is None else out_im + im
    return out_re, out_im


def cprod(a, b):
    return a[0] * b[0] - a[1] * b[1], a[0] * b[1] + a[1] * b[0]


def kernel(x_hbm, u_ref, cz_ref, o_ref, z_ref,
           psi, abuf, bo, bf, xb, yb, cb, st, kl, ml, acc, tot, diff, fvec, gvec, msg,
           in_sem, ps, ar, bor, bfr, fs, os_, xs, xr, ys, yr, cs, cr_, vs, vr, ms, mr):
    me = lax.axis_index('q')
    z = me // 8
    sub = me % 8
    b = z // 2
    inner = jnp.logical_or(z == 1, z == 2)
    outer = jnp.logical_not(inner)
    dev_in = sub + 8 * (1 + b)
    dev_mid = jnp.where(inner, sub + 8 * (3 - z), dev_in)
    dev_out = jnp.where(inner, sub + 24 * b, dev_in)
    dev_x = me + 2 - 4 * ((me // 2) % 2)
    dev_y = me + 4 - 8 * ((me // 4) % 2)
    dev_c = me + 1 - 2 * (me % 2)

    def in_copy(c, slot):
        return pltpu.make_async_copy(x_hbm.at[pl.ds(pl.multiple_of(c * 2 * GR, 8), 2 * GR), :],
                                     st.at[pl.ds(pl.multiple_of(slot * 2 * GR, 8), 2 * GR), :], in_sem.at[slot])

    in_copy(0, 0).start()
    in_copy(8, 1).start()

    barrier = pltpu.get_barrier_semaphore()

    def greet(dev):
        pl.semaphore_signal(barrier, inc=1, device_id=(dev,), device_id_type=MESH)

    greet(dev_x)
    greet(dev_y)
    greet(dev_c)
    greet(dev_mid)

    @pl.when(inner)
    def _():
        greet(dev_out)
        pl.semaphore_wait(barrier, 5)

    @pl.when(outer)
    def _():
        pl.semaphore_wait(barrier, 4)

    def u(q, i, j):
        return u_ref[0, i, j, q], u_ref[1, i, j, q]

    def gate(q):
        return (u(q, 0, 0), u(q, 0, 1)), (u(q, 1, 0), u(q, 1, 1))

    def apply_pair(g, p0, p1):
        return cmac(((g[0][0], p0), (g[0][1], p1))), cmac(((g[1][0], p0), (g[1][1], p1)))

    def rows(start, size):
        return pl.ds(pl.multiple_of(start, 8), size)

    def load(ref, start, size):
        return ref[0, rows(start, size), :], ref[1, rows(start, size), :]

    def store(ref, start, size, val):
        ref[0, rows(start, size), :] = val[0]
        ref[1, rows(start, size), :] = val[1]

    def gslice(ref, c):
        return ref.at[:, rows(c * GR, GR), :]

    def remote(src, dst, ss, rs, dev):
        return pltpu.make_async_remote_copy(src_ref=src, dst_ref=dst, send_sem=ss, recv_sem=rs,
                                            device_id=(dev,), device_id_type=MESH)

    def zslice(ref, half, k):
        if half == 0:
            return ref.at[:, rows(k * GR, GR), :]
        return ref.at[:, rows(HALF + k * SR, SR), :]

    def own_copy(half, k):
        n = k + half * NF
        return remote(zslice(psi, half, k), zslice(bo, half, k), ps.at[n], bor.at[n], dev_mid)

    def up_copy(half, k):
        n = k + half * NF
        return remote(zslice(psi, half, k), zslice(abuf, half, k), ps.at[n], ar.at[n], dev_in)

    def fwd_copy(half, k):
        n = k + half * NF
        return remote(zslice(abuf, half, k), zslice(bf, half, k), fs.at[n], bfr.at[n], dev_mid)

    def down_copy(half, k):
        n = k + half * NF
        return remote(zslice(abuf, half, k), zslice(bo, half, k), os_.at[n], bor.at[n], dev_out)

    cd = u(0, b, b)
    co = u(0, b, 1 - b)
    w_own = (cprod(cd, u(1, 1 - b, 1 - b)), cprod(cd, u(1, 1 - b, b)),
             cprod(co, u(1, 1 - b, b)), cprod(co, u(1, 1 - b, 1 - b)))
    w_out = (cprod(cd, u(1, b, 1 - b)), cprod(cd, u(1, b, b)),
             cprod(co, u(1, b, b)), cprod(co, u(1, b, 1 - b)))

    def fold(d):
        t = d[0:8]
        for j in range(1, BLK // 8):
            t = t + d[8 * j:8 * j + 8]
        return t

    def finish_z(half, k):
        @pl.when(inner)
        def _():
            own_copy(half, k).wait_send()
            fwd_copy(half, k).wait_send()
            own_copy(half, k).wait_recv()
            fwd_copy(half, k).wait_recv()
            if half:
                tot[NS + k] = jnp.zeros((8, LANES), jnp.float32)

            def body(i):
                s = (HALF + k * SR if half else k * GR) + i * BLK
                vals = (load(psi, s, BLK), load(abuf, s, BLK), load(bo, s, BLK), load(bf, s, BLK))
                own = cmac(tuple(zip(w_own, vals)))
                out = cmac(tuple(zip(w_out, vals)))
                store(abuf, s, BLK, out)
                store(bo, s, BLK, own)
                if half:
                    d_own = own[0] * own[0] + own[1] * own[1]
                    d_out = out[0] * out[0] + out[1] * out[1]
                    acc[rows(i * BLK, BLK), :] += d_own + d_out
                    tot[NS + k] += fold(d_own + d_out)
                    diff[...] += fold(d_own - d_out)
            loop((SR if half else GR) // BLK, body)
            down_copy(half, k).start()

        @pl.when(outer)
        def _():
            up_copy(half, k).wait_send()
            down_copy(half, k).wait_recv()

    def xchg(state, c, stage):
        buf, ss, rs, dev = ((xb, xs, xr, dev_x), (yb, ys, yr, dev_y), (cb, cs, cr_, dev_c))[stage]
        return remote(gslice(state, c), gslice(buf, c % 8), ss.at[c], rs.at[c], dev)

    bits = ((me // 2) % 2, (me // 4) % 2, me % 2)
    mix_coef = tuple((u(q, v, v), u(q, v, 1 - v)) for q, v in zip((3, 2, 4), bits))

    def mix(state, c, stage):
        cp = xchg(state, c, stage)
        cp.wait_send()
        cp.wait_recv()
        other = (xb, yb, cb)[stage]
        coef = mix_coef[stage]

        def body(i):
            s = c * GR + i * BLK
            t = (c % 8) * GR + i * BLK
            store(state, s, BLK, cmac(((coef[0], load(state, s, BLK)), (coef[1], load(other, t, BLK)))))
        loop(GR // BLK, body, unroll=2)

    g9 = gate(9)
    g10 = gate(10)

    def local_gates(state, c):
        base = c * GR

        def rowgates(i):
            p = [load(state, base + j * 128 + i * 16, 16) for j in range(4)]
            p[0], p[2] = apply_pair(g9, p[0], p[2])
            p[1], p[3] = apply_pair(g9, p[1], p[3])
            p[0], p[1] = apply_pair(g10, p[0], p[1])
            p[2], p[3] = apply_pair(g10, p[2], p[3])
            for j in range(4):
                store(state, base + j * 128 + i * 16, 16, p[j])
        loop(8, rowgates)

        def mats(h):
            s = base + h * 256
            a = load(state, s, 128)
            d = load(state, s + 128, 128)
            packed = jnp.concatenate([jnp.concatenate([a[0], d[0]], axis=1),
                                      jnp.concatenate([a[1], d[1]], axis=1)], axis=0)
            m = jnp.dot(ml[...], packed, precision=HIGHEST, preferred_element_type=jnp.float32)
            packed = jnp.concatenate([jnp.concatenate([m[:128, :128], m[128:, :128]], axis=1),
                                      jnp.concatenate([m[:128, 128:], m[128:, 128:]], axis=1)], axis=0)
            m = jnp.dot(packed, kl[...], precision=HIGHEST, preferred_element_type=jnp.float32)
            store(state, s, 256, (m[:, :128], m[:, 128:]))
        loop(2, mats)

    g678 = (gate(6), gate(7), gate(8))

    def chunk_gates(state, first_row):
        def body(i):
            p = [load(state, first_row + j * GR + i * 8, 8) for j in range(8)]
            for g, step in zip(g678, (4, 2, 1)):
                for j in range(8):
                    if not j & step:
                        p[j], p[j + step] = apply_pair(g, p[j], p[j + step])
            for j in range(8):
                store(state, first_row + j * GR + i * 8, 8, p[j])
        loop(GR // 8, body)

    g5 = gate(5)

    def phase0(c):
        slot = 2 * (c % 2)
        nxt = 2 - slot

        @pl.when(c < 7)
        def _():
            in_copy(c + 1, nxt).start()
            in_copy(c + 9, nxt + 1).start()
        in_copy(c, slot).wait()
        in_copy(c + 8, slot + 1).wait()

        def body(i):
            s0 = slot * 2 * GR + i * 2 * BLK
            s1_ = s0 + 2 * GR
            lo = st[pl.ds(s0, BLK, stride=2), :], st[pl.ds(s0 + 1, BLK, stride=2), :]
            hi = st[pl.ds(s1_, BLK, stride=2), :], st[pl.ds(s1_ + 1, BLK, stride=2), :]
            n0, n1 = apply_pair(g5, lo, hi)
            store(psi, c * GR + i * BLK, BLK, n0)
            store(psi, (c + 8) * GR + i * BLK, BLK, n1)
        loop(GR // BLK, body)

        @pl.when(inner)
        def _():
            own_copy(0, c).start()

        @pl.when(outer)
        def _():
            up_copy(0, c).start()
    loop(8, phase0)

    row = lax.broadcasted_iota(jnp.int32, (128, 128), 0)
    col = lax.broadcasted_iota(jnp.int32, (128, 128), 1)

    def kron(first, out_idx, in_idx):
        val = None
        for j in range(7):
            g = gate(first + j)
            ob = ((out_idx >> (6 - j)) & 1) == 1
            ib = ((in_idx >> (6 - j)) & 1) == 1
            f = tuple(jnp.where(ob, jnp.where(ib, g[1][1][r], g[1][0][r]), jnp.where(ib, g[0][1][r], g[0][0][r]))
                      for r in range(2))
            val = f if val is None else cprod(val, f)
        return val
    km = kron(18, col, row)
    kl[0:128, 0:128] = km[0]
    kl[0:128, 128:256] = km[1]
    kl[128:256, 0:128] = -km[1]
    kl[128:256, 128:256] = km[0]
    mm = kron(11, row, col)
    ml[0:128, 0:128] = mm[0]
    ml[0:128, 128:256] = -mm[1]
    ml[128:256, 0:128] = mm[1]
    ml[128:256, 128:256] = mm[0]
    chunk_gates(psi, HALF)

    def phase2(i):
        @pl.when(i < 8)
        def _():
            local_gates(psi, 8 + i)
            xchg(psi, 8 + i, 0).start()

            @pl.when(inner)
            def _():
                up_copy(0, i).wait_recv()
                fwd_copy(0, i).start()

        @pl.when(jnp.logical_and(i >= 1, i < 9))
        def _():
            mix(psi, 7 + i, 0)
            xchg(psi, 7 + i, 1).start()

        @pl.when(jnp.logical_and(i >= 2, i < 10))
        def _():
            mix(psi, 6 + i, 1)
            xchg(psi, 6 + i, 2).start()

        @pl.when(i >= 3)
        def _():
            mix(psi, 5 + i, 2)

            @pl.when(outer)
            def _():
                for j in range(4):
                    up_copy(1, 4 * (i - 3) + j).start()
    loop(11, phase2)

    def phase3(i):
        @pl.when(i < 8)
        def _():
            @pl.when(inner)
            def _():
                for j in range(4):
                    own_copy(1, 4 * i + j).start()
                    up_copy(1, 4 * i + j).wait_recv()
                    fwd_copy(1, 4 * i + j).start()
            finish_z(0, i)
            local_gates(bo, i)
            xchg(bo, i, 0).start()

        @pl.when(jnp.logical_and(i >= 1, i < 9))
        def _():
            mix(bo, i - 1, 0)
            xchg(bo, i - 1, 1).start()

        @pl.when(jnp.logical_and(i >= 2, i < 10))
        def _():
            mix(bo, i - 2, 1)
            xchg(bo, i - 2, 2).start()

        @pl.when(i >= 3)
        def _():
            mix(bo, i - 3, 2)
    loop(11, phase3)

    chunk_gates(bo, 0)
    flat = lax.broadcasted_iota(jnp.int32, (BLK, LANES), 0) * LANES + lax.broadcasted_iota(jnp.int32, (BLK, LANES), 1)
    shifts = [(NQ - 1 - cz_ref[0, p], NQ - 1 - cz_ref[1, p]) for p in range(12)]

    def emit(half, k):
        if not half:
            tot[k] = jnp.zeros((8, LANES), jnp.float32)

        def body(i):
            s = half * HALF + k * SR + i * BLK
            re, im = load(bo, s, BLK)
            idx = flat + (me * (ROWS * LANES) + s * LANES)
            par = None
            for sa, sb in shifts:
                t = lax.shift_right_logical(idx, sa) & lax.shift_right_logical(idx, sb)
                par = t if par is None else par ^ t
            sign = (1 - 2 * (par & 1)).astype(jnp.float32)
            if not half:
                d = re * re + im * im
                acc[rows(i * BLK, BLK), :] += d
                tot[k] += fold(d)
            o_ref[pl.ds(2 * s, BLK, stride=2), :] = re * sign
            o_ref[pl.ds(2 * s + 1, BLK, stride=2), :] = im * sign
        loop(SR // BLK, body)

    sl = lax.broadcasted_iota(jnp.int32, (8, LANES), 0)
    ln = lax.broadcasted_iota(jnp.int32, (8, LANES), 1)

    def sgn(bit):
        return (1 - 2 * bit).astype(jnp.float32)

    def signed(terms, bit):
        parts = [-t if (v >> bit) & 1 else t for v, t in enumerate(terms)]
        while len(parts) > 1:
            parts = [parts[v] + parts[v + 1] for v in range(0, len(parts), 2)]
        return parts[0]

    def sums(half):
        units = [tot[half * NS + v] for v in range(NS)]
        total = signed([t for t in units], 30)
        wide = [acc[8 * v:8 * v + 8, :] for v in range(SR // 8)]
        vecs = [total * sgn(b)]
        vecs.append(diff[...] * -sgn(b) if half else total * sgn(z % 2))
        vecs += [total * sgn((me // 2 ** (4 - q)) % 2) for q in range(2, 5)]
        vecs.append(-total if half else total)
        vecs += [signed(units, 10 - q) for q in range(6, 11)]
        vecs += [signed(wide, 14 - q) for q in range(11, 15)]
        vecs += [total * sgn((sl >> (17 - q)) & 1) for q in range(15, 18)]
        vecs += [total * sgn((ln >> (24 - q)) & 1) for q in range(18, 25)]
        parts = [jnp.sum(v, axis=0, keepdims=True) for v in vecs]
        return jnp.concatenate(parts + [jnp.zeros((1, LANES), jnp.float32)] * (32 - NQ), axis=0)

    acc[...] = jnp.zeros_like(acc)
    loop(NS, lambda k: emit(0, k))
    fvec[...] = sums(0)
    up_sums = remote(fvec, gvec, vs, vr, dev_in)

    @pl.when(outer)
    def _():
        up_sums.start()

    @pl.when(inner)
    def _():
        up_sums.wait_recv()
        fvec[...] += gvec[...]
        acc[...] = jnp.zeros_like(acc)
        diff[...] = jnp.zeros_like(diff)

    def phase5(j):
        finish_z(1, j)
        emit(1, j)
    loop(NS - 1, phase5)
    finish_z(1, NS - 1)

    mine = b * 8 + sub

    def msg_copy(r):
        return remote(msg.at[mine], msg.at[mine], ms.at[r], mr.at[mine], (me + r) % 32)

    @pl.when(inner)
    def _():
        wide = jnp.concatenate([fvec[...] + sums(1), jnp.zeros((LANES - 32, LANES), jnp.float32)], axis=0)
        msg[pl.ds(mine, 1)] = jnp.sum(wide.T, axis=0, keepdims=True)[None]
        loop(31, lambda r: msg_copy(r + 1).start())
    emit(1, NS - 1)

    @pl.when(inner)
    def _():
        loop(NF, lambda k: down_copy(0, k).wait_send())
        loop(NS, lambda k: down_copy(1, k).wait_send())

    @pl.when(outer)
    def _():
        up_sums.wait_send()

    def receive(t):
        dev = t % 8 + 8 * (1 + t // 8)

        @pl.when(dev != me)
        def _():
            remote(msg.at[t], msg.at[t], ms.at[0], mr.at[t], dev).wait_recv()
    loop(16, receive)
    val = msg[0]
    for t in range(1, 16):
        val = val + msg[t]
    z_ref[...] = (val * (1.0 / (ROWS * LANES * 32)))[:, :NQ]

    @pl.when(inner)
    def _():
        loop(31, lambda r: msg_copy(r + 1).wait_send())


def solution(mesh):
    dma = pltpu.SemaphoreType.DMA
    big = pltpu.VMEM((2, ROWS, LANES), jnp.float32)
    half = pltpu.VMEM((2, HALF, LANES), jnp.float32)

    def local_layer(state_local, unitaries, cz_pairs):
        x = state_local.reshape(2, ROWS, LANES).transpose(1, 0, 2).reshape(2 * ROWS, LANES)
        gates = unitaries.transpose(0, 2, 3, 1)
        out, z_exp = pl.pallas_call(
            kernel,
            name="gate_layer",
            out_shape=(pltpu.VMEM((2 * ROWS, LANES), jnp.float32), pltpu.VMEM((1, NQ), jnp.float32)),
            in_specs=[pl.BlockSpec(memory_space=pl.ANY),
                      pl.BlockSpec(memory_space=pltpu.SMEM),
                      pl.BlockSpec(memory_space=pltpu.SMEM)],
            out_specs=(pl.BlockSpec(memory_space=pltpu.VMEM), pl.BlockSpec(memory_space=pltpu.VMEM)),
            scratch_shapes=[big] * 4 + [half] * 3 + [
                pltpu.VMEM((4 * 2 * GR, LANES), jnp.float32),
                pltpu.VMEM((256, 256), jnp.float32),
                pltpu.VMEM((256, 256), jnp.float32),
                pltpu.VMEM((SR, LANES), jnp.float32),
                pltpu.VMEM((2 * NS, 8, LANES), jnp.float32),
                pltpu.VMEM((8, LANES), jnp.float32),
                pltpu.VMEM((32, LANES), jnp.float32),
                pltpu.VMEM((32, LANES), jnp.float32),
                pltpu.VMEM((16, 1, LANES), jnp.float32),
                dma((4,))] + [dma((NF + NS,))] * 6 + [dma((NG,))] * 6 + [
                dma(()), dma(()), dma((32,)), dma((16,))],
            compiler_params=pltpu.CompilerParams(has_side_effects=True, collective_id=0,
                                                 vmem_limit_bytes=VMEM_LIMIT),
        )(x, gates, cz_pairs.transpose(1, 0))
        out = out.reshape(ROWS, 2, LANES).transpose(1, 0, 2).reshape(2, ROWS * LANES)
        return out, z_exp.reshape(NQ)

    return jax.shard_map(local_layer, mesh=mesh, in_specs=(P(None, 'q'), P(), P()),
                         out_specs=(P(None, 'q'), P()), check_vma=False)
```

time: 401 us -> 381 us (0.950)
  Pallas kernels: 392 us -> 376 us
    pallas_call x1, Pallas kernels: 392 us -> 376 us  [local_layer(): pl.pallas_call(kernel, name='gate_layer', out_shape=(pltpu.VMEM((2 * ROWS...]
where the time goes in v2:
time: 381 us
  Pallas kernels  376 us (99%)
  local copies, waits for them, and re-layouts  3.91 us (1%)
    pallas_call x1, Pallas kernels, local_layer(): pl.pallas_call(kernel, name='gate_layer', out_shape=(pltpu.VMEM((2 * ROWS...  376 us

profile of v2, /device:TPU:0, one launch (start us, length us, event | category | flops | bytes accessed | tf_op | source)
XLA Modules:
  0.0 380.5 jit_solution(17668573757314933284)
XLA Ops:
  0.6 376.0 %gate_layer.1 = (f32[16384,128]{1,0:T(8,128)S(1)}, f32[1,25]{1,0:T(1,128)S(1)}) custom-call(f32[16384,128]{1,0:T(8,128)} %bitcast.15, f32[2,2,2,25]{3,2,1,0:T(2,128)} %bitcast.16, s32[2,12]{1,0:T(2,128)} %bitcast.17), custom_call_target="tpu_custom_call" | custom-call | tf_op jit(solution)/shard_map/gate_layer/pallas_call | solution.py:476
  376.6 3.4 copy.9
  380.0 0.5 copy.10

commit v3 on v2

--- a/solution.py
+++ b/solution.py
@@ -11,11 +11,14 @@
 NG = 16
 GR = ROWS // NG
 NF = 8
+NT = 8
+TR = GR // NT
+SR = 128
 NS = 32
-SR = 128
 HALF = ROWS // 2
 BLK = 32
 NQ = 25
+NW = 8
 HIGHEST = lax.Precision.HIGHEST
 VMEM_LIMIT = 50 * 2 ** 20
 
@@ -42,9 +45,9 @@
     return a[0] * b[0] - a[1] * b[1], a[0] * b[1] + a[1] * b[0]
 
 
-def kernel(x_hbm, u_ref, cz_ref, o_ref, z_ref,
-           psi, abuf, bo, bf, xb, yb, cb, st, kl, ml, acc, tot, diff, fvec, gvec, msg,
-           in_sem, ps, ar, bor, bfr, fs, os_, xs, xr, ys, yr, cs, cr_, vs, vr, ms, mr):
+def kernel(x_hbm, u_hbm, cz_hbm, o_ref, z_ref,
+           psi, abuf, bo, bf, xb, yb, cb, st, kl, ml, acc, tot, diff, fvec, gvec, msg, sent, u_ref, cz_ref,
+           par_sem, in_sem, ps, ar, bor, bfr, fs, os_, xs, xr, ys, yr, cs, cr_, vs, vr, ms, mr):
     me = lax.axis_index('q')
     z = me // 8
     sub = me % 8
@@ -62,9 +65,6 @@
         return pltpu.make_async_copy(x_hbm.at[pl.ds(pl.multiple_of(c * 2 * GR, 8), 2 * GR), :],
                                      st.at[pl.ds(pl.multiple_of(slot * 2 * GR, 8), 2 * GR), :], in_sem.at[slot])
 
-    in_copy(0, 0).start()
-    in_copy(8, 1).start()
-
     barrier = pltpu.get_barrier_semaphore()
 
     def greet(dev):
@@ -78,6 +78,17 @@
     @pl.when(inner)
     def _():
         greet(dev_out)
+    u_copy = pltpu.make_async_copy(u_hbm, u_ref, par_sem.at[0])
+    cz_copy = pltpu.make_async_copy(cz_hbm, cz_ref, par_sem.at[1])
+    u_copy.start()
+    in_copy(0, 0).start()
+    in_copy(8, 1).start()
+    cz_copy.start()
+    u_copy.wait()
+    cz_copy.wait()
+
+    @pl.when(inner)
+    def _():
         pl.semaphore_wait(barrier, 5)
 
     @pl.when(outer)
@@ -110,26 +121,28 @@
         return pltpu.make_async_remote_copy(src_ref=src, dst_ref=dst, send_sem=ss, recv_sem=rs,
                                             device_id=(dev,), device_id_type=MESH)
 
-    def zslice(ref, half, k):
-        if half == 0:
-            return ref.at[:, rows(k * GR, GR), :]
-        return ref.at[:, rows(HALF + k * SR, SR), :]
-
-    def own_copy(half, k):
-        n = k + half * NF
-        return remote(zslice(psi, half, k), zslice(bo, half, k), ps.at[n], bor.at[n], dev_mid)
-
-    def up_copy(half, k):
-        n = k + half * NF
-        return remote(zslice(psi, half, k), zslice(abuf, half, k), ps.at[n], ar.at[n], dev_in)
-
-    def fwd_copy(half, k):
-        n = k + half * NF
-        return remote(zslice(abuf, half, k), zslice(bf, half, k), fs.at[n], bfr.at[n], dev_mid)
-
-    def down_copy(half, k):
-        n = k + half * NF
-        return remote(zslice(abuf, half, k), zslice(bo, half, k), os_.at[n], bor.at[n], dev_out)
+    def span(kind, k):
+        if kind == 2:
+            return (NG - 1) * GR + k * TR, TR
+        return (kind * 8 + k) * GR, GR
+
+    def zslice(ref, kind, k):
+        return ref.at[:, rows(*span(kind, k)), :]
+
+    def index(kind, k):
+        return k + (0, 8, 15)[kind]
+
+    def own_copy(kind, k):
+        return remote(zslice(psi, kind, k), zslice(bo, kind, k), ps, bor.at[index(kind, k)], dev_mid)
+
+    def up_copy(kind, k):
+        return remote(zslice(psi, kind, k), zslice(abuf, kind, k), ps, ar.at[index(kind, k)], dev_in)
+
+    def fwd_copy(kind, k):
+        return remote(zslice(abuf, kind, k), zslice(bf, kind, k), fs, bfr.at[index(kind, k)], dev_mid)
+
+    def down_copy(kind, k):
+        return remote(zslice(bf, kind, k), zslice(bo, kind, k), os_, bor.at[index(kind, k)], dev_out)
 
     cd = u(0, b, b)
     co = u(0, b, 1 - b)
@@ -144,40 +157,37 @@
             t = t + d[8 * j:8 * j + 8]
         return t
 
-    def finish_z(half, k):
+    def finish_z(kind, k):
+        start, size = span(kind, k)
+
         @pl.when(inner)
         def _():
-            own_copy(half, k).wait_send()
-            fwd_copy(half, k).wait_send()
-            own_copy(half, k).wait_recv()
-            fwd_copy(half, k).wait_recv()
-            if half:
-                tot[NS + k] = jnp.zeros((8, LANES), jnp.float32)
+            own_copy(kind, k).wait_recv()
+            fwd_copy(kind, k).wait_recv()
 
             def body(i):
-                s = (HALF + k * SR if half else k * GR) + i * BLK
+                s = start + i * BLK
                 vals = (load(psi, s, BLK), load(abuf, s, BLK), load(bo, s, BLK), load(bf, s, BLK))
                 own = cmac(tuple(zip(w_own, vals)))
                 out = cmac(tuple(zip(w_out, vals)))
-                store(abuf, s, BLK, out)
+                store(bf, s, BLK, out)
                 store(bo, s, BLK, own)
-                if half:
+                if kind:
                     d_own = own[0] * own[0] + own[1] * own[1]
                     d_out = out[0] * out[0] + out[1] * out[1]
-                    acc[rows(i * BLK, BLK), :] += d_own + d_out
-                    tot[NS + k] += fold(d_own + d_out)
+                    acc[rows(s % SR, BLK), :] += d_own + d_out
+                    tot[s // SR] += fold(d_own + d_out)
                     diff[...] += fold(d_own - d_out)
-            loop((SR if half else GR) // BLK, body)
-            down_copy(half, k).start()
+            loop(size // BLK, body)
+            down_copy(kind, k).start()
 
         @pl.when(outer)
         def _():
-            up_copy(half, k).wait_send()
-            down_copy(half, k).wait_recv()
+            down_copy(kind, k).wait_recv()
 
     def xchg(state, c, stage):
         buf, ss, rs, dev = ((xb, xs, xr, dev_x), (yb, ys, yr, dev_y), (cb, cs, cr_, dev_c))[stage]
-        return remote(gslice(state, c), gslice(buf, c % 8), ss.at[c], rs.at[c], dev)
+        return remote(gslice(state, c), gslice(buf, c % 8), ss.at[c % 2], rs.at[c % 8], dev)
 
     bits = ((me // 2) % 2, (me // 4) % 2, me % 2)
     mix_coef = tuple((u(q, v, v), u(q, v, 1 - v)) for q, v in zip((3, 2, 4), bits))
@@ -321,8 +331,7 @@
 
             @pl.when(outer)
             def _():
-                for j in range(4):
-                    up_copy(1, 4 * (i - 3) + j).start()
+                up_copy(1, i - 3).start()
     loop(11, phase2)
 
     def phase3(i):
@@ -330,10 +339,18 @@
         def _():
             @pl.when(inner)
             def _():
-                for j in range(4):
-                    own_copy(1, 4 * i + j).start()
-                    up_copy(1, 4 * i + j).wait_recv()
-                    fwd_copy(1, 4 * i + j).start()
+                @pl.when(i < 7)
+                def _():
+                    own_copy(1, i).start()
+                    up_copy(1, i).wait_recv()
+                    fwd_copy(1, i).start()
+
+                @pl.when(i == 7)
+                def _():
+                    up_copy(1, 7).wait_recv()
+                    for j in range(NT):
+                        own_copy(2, j).start()
+                        fwd_copy(2, j).start()
             finish_z(0, i)
             local_gates(bo, i)
             xchg(bo, i, 0).start()
@@ -357,12 +374,11 @@
     flat = lax.broadcasted_iota(jnp.int32, (BLK, LANES), 0) * LANES + lax.broadcasted_iota(jnp.int32, (BLK, LANES), 1)
     shifts = [(NQ - 1 - cz_ref[0, p], NQ - 1 - cz_ref[1, p]) for p in range(12)]
 
-    def emit(half, k):
-        if not half:
-            tot[k] = jnp.zeros((8, LANES), jnp.float32)
+    def emit(kind, k):
+        start, size = span(kind, k)
 
         def body(i):
-            s = half * HALF + k * SR + i * BLK
+            s = start + i * BLK
             re, im = load(bo, s, BLK)
             idx = flat + (me * (ROWS * LANES) + s * LANES)
             par = None
@@ -370,13 +386,13 @@
                 t = lax.shift_right_logical(idx, sa) & lax.shift_right_logical(idx, sb)
                 par = t if par is None else par ^ t
             sign = (1 - 2 * (par & 1)).astype(jnp.float32)
-            if not half:
+            if not kind:
                 d = re * re + im * im
-                acc[rows(i * BLK, BLK), :] += d
-                tot[k] += fold(d)
+                acc[rows(s % SR, BLK), :] += d
+                tot[s // SR] += fold(d)
             o_ref[pl.ds(2 * s, BLK, stride=2), :] = re * sign
             o_ref[pl.ds(2 * s + 1, BLK, stride=2), :] = im * sign
-        loop(SR // BLK, body)
+        loop(size // BLK, body)
 
     sl = lax.broadcasted_iota(jnp.int32, (8, LANES), 0)
     ln = lax.broadcasted_iota(jnp.int32, (8, LANES), 1)
@@ -406,7 +422,8 @@
         return jnp.concatenate(parts + [jnp.zeros((1, LANES), jnp.float32)] * (32 - NQ), axis=0)
 
     acc[...] = jnp.zeros_like(acc)
-    loop(NS, lambda k: emit(0, k))
+    tot[...] = jnp.zeros_like(tot)
+    loop(8, lambda k: emit(0, k))
     fvec[...] = sums(0)
     up_sums = remote(fvec, gvec, vs, vr, dev_in)
 
@@ -421,39 +438,41 @@
         acc[...] = jnp.zeros_like(acc)
         diff[...] = jnp.zeros_like(diff)
 
-    def phase5(j):
-        finish_z(1, j)
-        emit(1, j)
-    loop(NS - 1, phase5)
-    finish_z(1, NS - 1)
+    def phase5(kind, k):
+        finish_z(kind, k)
+        emit(kind, k)
+    loop(7, lambda k: phase5(1, k))
+    loop(NT - 1, lambda k: phase5(2, k))
+    finish_z(2, NT - 1)
 
     mine = b * 8 + sub
 
     def msg_copy(r):
-        return remote(msg.at[mine], msg.at[mine], ms.at[r], mr.at[mine], (me + r) % 32)
+        return remote(msg.at[mine], msg.at[mine], ms, mr.at[mine], (me + r) % 32)
 
     @pl.when(inner)
     def _():
         wide = jnp.concatenate([fvec[...] + sums(1), jnp.zeros((LANES - 32, LANES), jnp.float32)], axis=0)
         msg[pl.ds(mine, 1)] = jnp.sum(wide.T, axis=0, keepdims=True)[None]
         loop(31, lambda r: msg_copy(r + 1).start())
-    emit(1, NS - 1)
+    emit(2, NT - 1)
 
     @pl.when(inner)
     def _():
-        loop(NF, lambda k: down_copy(0, k).wait_send())
-        loop(NS, lambda k: down_copy(1, k).wait_send())
+        remote(abuf, bf, fs, vr, dev_mid).wait_send()
+        remote(bf, bo, os_, vr, dev_out).wait_send()
 
     @pl.when(outer)
     def _():
         up_sums.wait_send()
+    remote(psi, bo, ps, vr, dev_mid).wait_send()
 
     def receive(t):
         dev = t % 8 + 8 * (1 + t // 8)
 
         @pl.when(dev != me)
         def _():
-            remote(msg.at[t], msg.at[t], ms.at[0], mr.at[t], dev).wait_recv()
+            remote(msg.at[t], msg.at[t], ms, mr.at[t], dev).wait_recv()
     loop(16, receive)
     val = msg[0]
     for t in range(1, 16):
@@ -462,7 +481,17 @@
 
     @pl.when(inner)
     def _():
-        loop(31, lambda r: msg_copy(r + 1).wait_send())
+        remote(sent, sent, ms, vr, dev_mid).wait_send()
+
+
+def writer(s_ref, z_ref, o_hbm, zo_ref, sem):
+    copies = [pltpu.make_async_copy(s_ref.at[pl.ds(k * 2 * ROWS // NW, 2 * ROWS // NW), :],
+                                    o_hbm.at[pl.ds(k * 2 * ROWS // NW, 2 * ROWS // NW), :], sem.at[k]) for k in range(NW)]
+    for cp in copies:
+        cp.start()
+    zo_ref[...] = z_ref[...]
+    for cp in copies:
+        cp.wait()
 
 
 def solution(mesh):
@@ -478,8 +507,8 @@
             name="gate_layer",
             out_shape=(pltpu.VMEM((2 * ROWS, LANES), jnp.float32), pltpu.VMEM((1, NQ), jnp.float32)),
             in_specs=[pl.BlockSpec(memory_space=pl.ANY),
-                      pl.BlockSpec(memory_space=pltpu.SMEM),
-                      pl.BlockSpec(memory_space=pltpu.SMEM)],
+                      pl.BlockSpec(memory_space=pl.ANY),
+                      pl.BlockSpec(memory_space=pl.ANY)],
             out_specs=(pl.BlockSpec(memory_space=pltpu.VMEM), pl.BlockSpec(memory_space=pltpu.VMEM)),
             scratch_shapes=[big] * 4 + [half] * 3 + [
                 pltpu.VMEM((4 * 2 * GR, LANES), jnp.float32),
@@ -491,11 +520,23 @@
                 pltpu.VMEM((32, LANES), jnp.float32),
                 pltpu.VMEM((32, LANES), jnp.float32),
                 pltpu.VMEM((16, 1, LANES), jnp.float32),
-                dma((4,))] + [dma((NF + NS,))] * 6 + [dma((NG,))] * 6 + [
-                dma(()), dma(()), dma((32,)), dma((16,))],
+                pltpu.VMEM((31, 1, LANES), jnp.float32),
+                pltpu.SMEM((2, 2, 2, NQ), jnp.float32),
+                pltpu.SMEM((2, 12), jnp.int32),
+                dma((2,)), dma((4,)), dma(()), dma((16,)), dma((15 + NT,)), dma((15 + NT,)), dma(()), dma(())] + [
+                dma((2,)), dma((8,))] * 3 + [dma(()), dma(()), dma(()), dma((16,))],
             compiler_params=pltpu.CompilerParams(has_side_effects=True, collective_id=0,
                                                  vmem_limit_bytes=VMEM_LIMIT),
         )(x, gates, cz_pairs.transpose(1, 0))
+        out, z_exp = pl.pallas_call(
+            writer,
+            name="write_result",
+            out_shape=(jax.ShapeDtypeStruct((2 * ROWS, LANES), jnp.float32), jax.ShapeDtypeStruct((1, NQ), jnp.float32)),
+            in_specs=[pl.BlockSpec(memory_space=pltpu.VMEM), pl.BlockSpec(memory_space=pltpu.VMEM)],
+            out_specs=(pl.BlockSpec(memory_space=pl.ANY), pl.BlockSpec(memory_space=pltpu.VMEM)),
+            scratch_shapes=[dma((NW,))],
+            compiler_params=pltpu.CompilerParams(vmem_limit_bytes=2 ** 20),
+        )(out, z_exp)
         out = out.reshape(ROWS, 2, LANES).transpose(1, 0, 2).reshape(2, ROWS * LANES)
         return out, z_exp.reshape(NQ)
 

time: 381 us -> 377 us (0.990)
  local copies, waits for them, and re-layouts: 3.91 us -> 0 us
    pallas_call x1, Pallas kernels: 376 us -> 372 us  [local_layer(): pl.pallas_call(kernel, name='gate_layer', out_shape=(pltpu.VMEM((2 * ROWS...]
    unnamed x2 -> x0, local copies, waits for them, and re-layouts: 3.91 us -> none
    pallas_call x0 -> x1, Pallas kernels: none -> 3.88 us  [local_layer(): pl.pallas_call(writer, name='write_result', out_shape=(jax.ShapeDtypeStru...]
where the time goes in v3:
time: 377 us
  Pallas kernels  376 us (100%)
    pallas_call x1, Pallas kernels, local_layer(): pl.pallas_call(kernel, name='gate_layer', out_shape=(pltpu.VMEM((2 * ROWS...  372 us

profile of v3, /device:TPU:0, one launch (start us, length us, event | category | flops | bytes accessed | tf_op | source)
XLA Modules:
  0.0 376.5 jit_solution(5750688377398447575)
XLA Ops:
  0.6 372.0 %gate_layer.1 = (f32[16384,128]{1,0:T(8,128)S(1)}, f32[1,25]{1,0:T(1,128)S(1)}) custom-call(f32[16384,128]{1,0:T(8,128)} %bitcast.13, f32[2,2,2,25]{3,2,1,0:T(2,128)} %bitcast.14, s32[2,12]{1,0:T(2,128)} %bitcast.15), custom_call_target="tpu_custom_call" | custom-call | tf_op jit(solution)/shard_map/gate_layer/pallas_call | solution.py:505
  372.6 3.9 %write_result.1 = (f32[16384,128]{1,0:T(8,128)}, f32[1,25]{1,0:T(1,128)}) custom-call(f32[16384,128]{1,0:T(8,128)S(1)} %get-tuple-element.6.s_ref, f32[1,25]{1,0:T(1,128)S(1)} %get-tuple-element.7.z_ref), custom_call_target="tpu_custom_call" | custom-call | tf_op jit(solution)/shard_map/write_result/pallas_call | solution.py:531

commit v4 on v3

--- a/solution.py
+++ b/solution.py
@@ -11,7 +11,7 @@
 NG = 16
 GR = ROWS // NG
 NF = 8
-NT = 8
+NT = 16
 TR = GR // NT
 SR = 128
 NS = 32
@@ -19,6 +19,9 @@
 BLK = 32
 NQ = 25
 NW = 8
+NX = 4
+LO = slice(0, 128)
+HI = slice(128, 256)
 HIGHEST = lax.Precision.HIGHEST
 VMEM_LIMIT = 50 * 2 ** 20
 
@@ -42,7 +45,12 @@
 
 
 def cprod(a, b):
-    return a[0] * b[0] - a[1] * b[1], a[0] * b[1] + a[1] * b[0]
+    return cmac(((a, b),))
+
+
+def norm2(a):
+    re, im = a
+    return re * re + im * im
 
 
 def kernel(x_hbm, u_hbm, cz_hbm, o_ref, z_ref,
@@ -57,9 +65,11 @@
     dev_in = sub + 8 * (1 + b)
     dev_mid = jnp.where(inner, sub + 8 * (3 - z), dev_in)
     dev_out = jnp.where(inner, sub + 24 * b, dev_in)
-    dev_x = me + 2 - 4 * ((me // 2) % 2)
-    dev_y = me + 4 - 8 * ((me // 4) % 2)
-    dev_c = me + 1 - 2 * (me % 2)
+
+    def my_bit(k):
+        return (me // 2 ** k) % 2
+
+    dev_c, dev_x, dev_y = [me + 2 ** k * (1 - 2 * my_bit(k)) for k in range(3)]
 
     def in_copy(c, slot):
         return pltpu.make_async_copy(x_hbm.at[pl.ds(pl.multiple_of(c * 2 * GR, 8), 2 * GR), :],
@@ -87,22 +97,14 @@
     u_copy.wait()
     cz_copy.wait()
 
-    @pl.when(inner)
-    def _():
-        pl.semaphore_wait(barrier, 5)
-
-    @pl.when(outer)
-    def _():
-        pl.semaphore_wait(barrier, 4)
-
     def u(q, i, j):
         return u_ref[0, i, j, q], u_ref[1, i, j, q]
 
     def gate(q):
-        return (u(q, 0, 0), u(q, 0, 1)), (u(q, 1, 0), u(q, 1, 1))
+        return tuple(tuple(u(q, i, j) for j in range(2)) for i in range(2))
 
     def apply_pair(g, p0, p1):
-        return cmac(((g[0][0], p0), (g[0][1], p1))), cmac(((g[1][0], p0), (g[1][1], p1)))
+        return tuple(cmac(tuple(zip(g_row, (p0, p1)))) for g_row in g)
 
     def rows(start, size):
         return pl.ds(pl.multiple_of(start, 8), size)
@@ -144,12 +146,12 @@
     def down_copy(kind, k):
         return remote(zslice(bf, kind, k), zslice(bo, kind, k), os_, bor.at[index(kind, k)], dev_out)
 
-    cd = u(0, b, b)
-    co = u(0, b, 1 - b)
-    w_own = (cprod(cd, u(1, 1 - b, 1 - b)), cprod(cd, u(1, 1 - b, b)),
-             cprod(co, u(1, 1 - b, b)), cprod(co, u(1, 1 - b, 1 - b)))
-    w_out = (cprod(cd, u(1, b, 1 - b)), cprod(cd, u(1, b, b)),
-             cprod(co, u(1, b, b)), cprod(co, u(1, b, 1 - b)))
+    def z_row(hi, lo):
+        return [cprod(u(0, hi, v), u(1, lo, w)) for v, w in ((b, 1 - b), (b, b), (1 - b, b), (1 - b, 1 - b))]
+    w_own = z_row(b, 1 - b)
+    w_out = z_row(b, b)
+    w_mid = z_row(1 - b, b)
+    w_far = z_row(1 - b, 1 - b)
 
     def fold(d):
         t = d[0:8]
@@ -157,7 +159,7 @@
             t = t + d[8 * j:8 * j + 8]
         return t
 
-    def finish_z(kind, k):
+    def finish_z(kind, k, count=2):
         start, size = span(kind, k)
 
         @pl.when(inner)
@@ -172,12 +174,20 @@
                 out = cmac(tuple(zip(w_out, vals)))
                 store(bf, s, BLK, out)
                 store(bo, s, BLK, own)
-                if kind:
-                    d_own = own[0] * own[0] + own[1] * own[1]
-                    d_out = out[0] * out[0] + out[1] * out[1]
-                    acc[rows(s % SR, BLK), :] += d_own + d_out
-                    tot[s // SR] += fold(d_own + d_out)
-                    diff[...] += fold(d_own - d_out)
+                if kind and count:
+                    d_own = norm2(own)
+                    d_out = norm2(out)
+                    near = d_own + d_out
+                    d0, d1 = near, d_own - d_out
+                    if count == 4:
+                        d_mid = norm2(cmac(tuple(zip(w_mid, vals))))
+                        d_far = norm2(cmac(tuple(zip(w_far, vals))))
+                        d0, d1 = near - (d_mid + d_far), d1 + (d_far - d_mid)
+                        near = near + (d_mid + d_far)
+                    acc[rows(s % SR, BLK), :] += near
+                    tot[s // SR] += fold(near)
+                    diff[0] += fold(d0)
+                    diff[1] += fold(d1)
             loop(size // BLK, body)
             down_copy(kind, k).start()
 
@@ -187,9 +197,9 @@
 
     def xchg(state, c, stage):
         buf, ss, rs, dev = ((xb, xs, xr, dev_x), (yb, ys, yr, dev_y), (cb, cs, cr_, dev_c))[stage]
-        return remote(gslice(state, c), gslice(buf, c % 8), ss.at[c % 2], rs.at[c % 8], dev)
-
-    bits = ((me // 2) % 2, (me // 4) % 2, me % 2)
+        return remote(gslice(state, c), gslice(buf, c % NX), ss.at[c % 2], rs.at[c % NX], dev)
+
+    bits = [my_bit(k) for k in (1, 2, 0)]
     mix_coef = tuple((u(q, v, v), u(q, v, 1 - v)) for q, v in zip((3, 2, 4), bits))
 
     def mix(state, c, stage):
@@ -201,7 +211,7 @@
 
         def body(i):
             s = c * GR + i * BLK
-            t = (c % 8) * GR + i * BLK
+            t = (c % NX) * GR + i * BLK
             store(state, s, BLK, cmac(((coef[0], load(state, s, BLK)), (coef[1], load(other, t, BLK)))))
         loop(GR // BLK, body, unroll=2)
 
@@ -213,10 +223,10 @@
 
         def rowgates(i):
             p = [load(state, base + j * 128 + i * 16, 16) for j in range(4)]
-            p[0], p[2] = apply_pair(g9, p[0], p[2])
-            p[1], p[3] = apply_pair(g9, p[1], p[3])
-            p[0], p[1] = apply_pair(g10, p[0], p[1])
-            p[2], p[3] = apply_pair(g10, p[2], p[3])
+            for g, step in ((g9, 2), (g10, 1)):
+                for j in range(4):
+                    if not j & step:
+                        p[j], p[j + step] = apply_pair(g, p[j], p[j + step])
             for j in range(4):
                 store(state, base + j * 128 + i * 16, 16, p[j])
         loop(8, rowgates)
@@ -225,13 +235,11 @@
             s = base + h * 256
             a = load(state, s, 128)
             d = load(state, s + 128, 128)
-            packed = jnp.concatenate([jnp.concatenate([a[0], d[0]], axis=1),
-                                      jnp.concatenate([a[1], d[1]], axis=1)], axis=0)
+            packed = jnp.concatenate([jnp.concatenate(pair, axis=1) for pair in zip(a, d)], axis=0)
             m = jnp.dot(ml[...], packed, precision=HIGHEST, preferred_element_type=jnp.float32)
-            packed = jnp.concatenate([jnp.concatenate([m[:128, :128], m[128:, :128]], axis=1),
-                                      jnp.concatenate([m[:128, 128:], m[128:, 128:]], axis=1)], axis=0)
+            packed = jnp.concatenate([jnp.concatenate([m[LO, h], m[HI, h]], axis=1) for h in (LO, HI)], axis=0)
             m = jnp.dot(packed, kl[...], precision=HIGHEST, preferred_element_type=jnp.float32)
-            store(state, s, 256, (m[:, :128], m[:, 128:]))
+            store(state, s, 256, (m[:, LO], m[:, HI]))
         loop(2, mats)
 
     g678 = (gate(6), gate(7), gate(8))
@@ -269,6 +277,14 @@
             store(psi, c * GR + i * BLK, BLK, n0)
             store(psi, (c + 8) * GR + i * BLK, BLK, n1)
         loop(GR // BLK, body)
+
+        @pl.when(jnp.logical_and(inner, c == 0))
+        def _():
+            pl.semaphore_wait(barrier, 5)
+
+        @pl.when(jnp.logical_and(outer, c == 0))
+        def _():
+            pl.semaphore_wait(barrier, 4)
 
         @pl.when(inner)
         def _():
@@ -293,15 +309,15 @@
             val = f if val is None else cprod(val, f)
         return val
     km = kron(18, col, row)
-    kl[0:128, 0:128] = km[0]
-    kl[0:128, 128:256] = km[1]
-    kl[128:256, 0:128] = -km[1]
-    kl[128:256, 128:256] = km[0]
+    kl[LO, LO] = km[0]
+    kl[LO, HI] = km[1]
+    kl[HI, LO] = -km[1]
+    kl[HI, HI] = km[0]
     mm = kron(11, row, col)
-    ml[0:128, 0:128] = mm[0]
-    ml[0:128, 128:256] = -mm[1]
-    ml[128:256, 0:128] = mm[1]
-    ml[128:256, 128:256] = mm[0]
+    ml[LO, LO] = mm[0]
+    ml[LO, HI] = -mm[1]
+    ml[HI, LO] = mm[1]
+    ml[HI, HI] = mm[0]
     chunk_gates(psi, HALF)
 
     def phase2(i):
@@ -348,9 +364,11 @@
                 @pl.when(i == 7)
                 def _():
                     up_copy(1, 7).wait_recv()
-                    for j in range(NT):
-                        own_copy(2, j).start()
-                        fwd_copy(2, j).start()
+                    def pieces(t):
+                        p = (t + b * (NT // 2)) % NT
+                        own_copy(2, p).start()
+                        fwd_copy(2, p).start()
+                    loop(NT, pieces)
             finish_z(0, i)
             local_gates(bo, i)
             xchg(bo, i, 0).start()
@@ -387,7 +405,7 @@
                 par = t if par is None else par ^ t
             sign = (1 - 2 * (par & 1)).astype(jnp.float32)
             if not kind:
-                d = re * re + im * im
+                d = norm2((re, im))
                 acc[rows(s % SR, BLK), :] += d
                 tot[s // SR] += fold(d)
             o_ref[pl.ds(2 * s, BLK, stride=2), :] = re * sign
@@ -410,9 +428,8 @@
         units = [tot[half * NS + v] for v in range(NS)]
         total = signed([t for t in units], 30)
         wide = [acc[8 * v:8 * v + 8, :] for v in range(SR // 8)]
-        vecs = [total * sgn(b)]
-        vecs.append(diff[...] * -sgn(b) if half else total * sgn(z % 2))
-        vecs += [total * sgn((me // 2 ** (4 - q)) % 2) for q in range(2, 5)]
+        vecs = [diff[0] * sgn(b), diff[1] * -sgn(b)] if half else [total * sgn(b), total * sgn(z % 2)]
+        vecs += [total * sgn(my_bit(4 - q)) for q in range(2, 5)]
         vecs.append(-total if half else total)
         vecs += [signed(units, 10 - q) for q in range(6, 11)]
         vecs += [signed(wide, 14 - q) for q in range(11, 15)]
@@ -438,12 +455,16 @@
         acc[...] = jnp.zeros_like(acc)
         diff[...] = jnp.zeros_like(diff)
 
-    def phase5(kind, k):
-        finish_z(kind, k)
-        emit(kind, k)
-    loop(7, lambda k: phase5(1, k))
-    loop(NT - 1, lambda k: phase5(2, k))
-    finish_z(2, NT - 1)
+    def phase5(k):
+        finish_z(1, k)
+        emit(1, k)
+    loop(7, phase5)
+
+    def tail(t, count):
+        p = (t + (1 - b) * (NT // 2)) % NT
+        finish_z(2, p, count)
+        emit(2, p)
+    loop(NT // 2, lambda t: tail(t, 4))
 
     mine = b * 8 + sub
 
@@ -455,17 +476,8 @@
         wide = jnp.concatenate([fvec[...] + sums(1), jnp.zeros((LANES - 32, LANES), jnp.float32)], axis=0)
         msg[pl.ds(mine, 1)] = jnp.sum(wide.T, axis=0, keepdims=True)[None]
         loop(31, lambda r: msg_copy(r + 1).start())
-    emit(2, NT - 1)
-
-    @pl.when(inner)
-    def _():
-        remote(abuf, bf, fs, vr, dev_mid).wait_send()
-        remote(bf, bo, os_, vr, dev_out).wait_send()
-
-    @pl.when(outer)
-    def _():
-        up_sums.wait_send()
-    remote(psi, bo, ps, vr, dev_mid).wait_send()
+
+    loop(NT // 2, lambda t: tail(t + NT // 2, 0))
 
     def receive(t):
         dev = t % 8 + 8 * (1 + t // 8)
@@ -481,15 +493,22 @@
 
     @pl.when(inner)
     def _():
+        remote(abuf, bf, fs, vr, dev_mid).wait_send()
         remote(sent, sent, ms, vr, dev_mid).wait_send()
+        remote(bf, bo, os_, vr, dev_out).wait_send()
+
+    @pl.when(outer)
+    def _():
+        up_sums.wait_send()
+    remote(psi, bo, ps, vr, dev_mid).wait_send()
 
 
 def writer(s_ref, z_ref, o_hbm, zo_ref, sem):
     copies = [pltpu.make_async_copy(s_ref.at[pl.ds(k * 2 * ROWS // NW, 2 * ROWS // NW), :],
                                     o_hbm.at[pl.ds(k * 2 * ROWS // NW, 2 * ROWS // NW), :], sem.at[k]) for k in range(NW)]
+    copies.append(pltpu.make_async_copy(z_ref, zo_ref, sem.at[NW]))
     for cp in copies:
         cp.start()
-    zo_ref[...] = z_ref[...]
     for cp in copies:
         cp.wait()
 
@@ -497,7 +516,7 @@
 def solution(mesh):
     dma = pltpu.SemaphoreType.DMA
     big = pltpu.VMEM((2, ROWS, LANES), jnp.float32)
-    half = pltpu.VMEM((2, HALF, LANES), jnp.float32)
+    slots = pltpu.VMEM((2, NX * GR, LANES), jnp.float32)
 
     def local_layer(state_local, unitaries, cz_pairs):
         x = state_local.reshape(2, ROWS, LANES).transpose(1, 0, 2).reshape(2 * ROWS, LANES)
@@ -510,13 +529,13 @@
                       pl.BlockSpec(memory_space=pl.ANY),
                       pl.BlockSpec(memory_space=pl.ANY)],
             out_specs=(pl.BlockSpec(memory_space=pltpu.VMEM), pl.BlockSpec(memory_space=pltpu.VMEM)),
-            scratch_shapes=[big] * 4 + [half] * 3 + [
+            scratch_shapes=[big] * 4 + [slots] * 3 + [
                 pltpu.VMEM((4 * 2 * GR, LANES), jnp.float32),
                 pltpu.VMEM((256, 256), jnp.float32),
                 pltpu.VMEM((256, 256), jnp.float32),
                 pltpu.VMEM((SR, LANES), jnp.float32),
                 pltpu.VMEM((2 * NS, 8, LANES), jnp.float32),
-                pltpu.VMEM((8, LANES), jnp.float32),
+                pltpu.VMEM((2, 8, LANES), jnp.float32),
                 pltpu.VMEM((32, LANES), jnp.float32),
                 pltpu.VMEM((32, LANES), jnp.float32),
                 pltpu.VMEM((16, 1, LANES), jnp.float32),
@@ -524,7 +543,7 @@
                 pltpu.SMEM((2, 2, 2, NQ), jnp.float32),
                 pltpu.SMEM((2, 12), jnp.int32),
                 dma((2,)), dma((4,)), dma(()), dma((16,)), dma((15 + NT,)), dma((15 + NT,)), dma(()), dma(())] + [
-                dma((2,)), dma((8,))] * 3 + [dma(()), dma(()), dma(()), dma((16,))],
+                dma((2,)), dma((NX,))] * 3 + [dma(()), dma(()), dma(()), dma((16,))],
             compiler_params=pltpu.CompilerParams(has_side_effects=True, collective_id=0,
                                                  vmem_limit_bytes=VMEM_LIMIT),
         )(x, gates, cz_pairs.transpose(1, 0))
@@ -533,8 +552,8 @@
             name="write_result",
             out_shape=(jax.ShapeDtypeStruct((2 * ROWS, LANES), jnp.float32), jax.ShapeDtypeStruct((1, NQ), jnp.float32)),
             in_specs=[pl.BlockSpec(memory_space=pltpu.VMEM), pl.BlockSpec(memory_space=pltpu.VMEM)],
-            out_specs=(pl.BlockSpec(memory_space=pl.ANY), pl.BlockSpec(memory_space=pltpu.VMEM)),
-            scratch_shapes=[dma((NW,))],
+            out_specs=(pl.BlockSpec(memory_space=pl.ANY), pl.BlockSpec(memory_space=pl.ANY)),
+            scratch_shapes=[dma((NW + 1,))],
             compiler_params=pltpu.CompilerParams(vmem_limit_bytes=2 ** 20),
         )(out, z_exp)
         out = out.reshape(ROWS, 2, LANES).transpose(1, 0, 2).reshape(2, ROWS * LANES)

time: 377 us -> 374 us (level)
  no operation moved by 1% of the time
where the time goes in v4:
time: 374 us
  Pallas kernels  373 us (100%)
    pallas_call x1, Pallas kernels, local_layer(): pl.pallas_call(kernel, name='gate_layer', out_shape=(pltpu.VMEM((2 * ROWS...  370 us

profile of v4, /device:TPU:0, one launch (start us, length us, event | category | flops | bytes accessed | tf_op | source)
XLA Modules:
  0.0 374.1 jit_solution(756156886493269693)
XLA Ops:
  0.6 370.0 %gate_layer.1 = (f32[16384,128]{1,0:T(8,128)S(1)}, f32[1,25]{1,0:T(1,128)S(1)}) custom-call(f32[16384,128]{1,0:T(8,128)} %bitcast.13, f32[2,2,2,25]{3,2,1,0:T(2,128)} %bitcast.14, s32[2,12]{1,0:T(2,128)} %bitcast.15), custom_call_target="tpu_custom_call" | custom-call | tf_op jit(solution)/shard_map/gate_layer/pallas_call | solution.py:524
  370.7 3.4 write_result.1

commit v5 on v4

--- a/solution.py
+++ b/solution.py
@@ -10,9 +10,13 @@
 ROWS = 8192
 NG = 16
 GR = ROWS // NG
-NF = 8
-NT = 16
-TR = GR // NT
+PIECES = (256, 256, 128, 128, 64, 32, 32)
+SIDE = GR // 2
+DR = 128
+DP = 64
+NT = len(PIECES)
+NZ = NG - 2 + NT
+FIRST = 128
 SR = 128
 NS = 32
 HALF = ROWS // 2
@@ -54,8 +58,8 @@
 
 
 def kernel(x_hbm, u_hbm, cz_hbm, o_ref, z_ref,
-           psi, abuf, bo, bf, xb, yb, cb, st, kl, ml, acc, tot, diff, fvec, gvec, msg, sent, u_ref, cz_ref,
-           par_sem, in_sem, ps, ar, bor, bfr, fs, os_, xs, xr, ys, yr, cs, cr_, vs, vr, ms, mr):
+           psi, abuf, bo, bf, xb, yb, cb, st, kl, ml, acc, tot, diff, fvec, gvec, msg, sent, pm, pf, rp, u_ref, cz_ref,
+           par_sem, in_sem, ps, ar, br, fs, os_, xs, xr, ys, yr, cs, cr_, vs, vr, ms, mr, er, dr):
     me = lax.axis_index('q')
     z = me // 8
     sub = me % 8
@@ -71,9 +75,15 @@
 
     dev_c, dev_x, dev_y = [me + 2 ** k * (1 - 2 * my_bit(k)) for k in range(3)]
 
-    def in_copy(c, slot):
-        return pltpu.make_async_copy(x_hbm.at[pl.ds(pl.multiple_of(c * 2 * GR, 8), 2 * GR), :],
-                                     st.at[pl.ds(pl.multiple_of(slot * 2 * GR, 8), 2 * GR), :], in_sem.at[slot])
+    def in_copy(c, slot, sem, start=0, size=GR):
+        return pltpu.make_async_copy(x_hbm.at[pl.ds(pl.multiple_of((c * GR + start) * 2, 8), 2 * size), :],
+                                     st.at[pl.ds(pl.multiple_of((slot * GR + start) * 2, 8), 2 * size), :], in_sem.at[sem])
+
+    def in_pair(c, slot, sem, start=0, size=GR):
+        return in_copy(c, slot, sem, start, size), in_copy(c + 8, slot + 1, sem + 1, start, size)
+
+    part_a = in_pair(0, 0, 0, 0, FIRST)
+    part_b = in_pair(0, 0, 2, FIRST, GR - FIRST)
 
     barrier = pltpu.get_barrier_semaphore()
 
@@ -91,11 +101,10 @@
     u_copy = pltpu.make_async_copy(u_hbm, u_ref, par_sem.at[0])
     cz_copy = pltpu.make_async_copy(cz_hbm, cz_ref, par_sem.at[1])
     u_copy.start()
-    in_copy(0, 0).start()
-    in_copy(8, 1).start()
+    for cp in part_a + part_b:
+        cp.start()
     cz_copy.start()
     u_copy.wait()
-    cz_copy.wait()
 
     def u(q, i, j):
         return u_ref[0, i, j, q], u_ref[1, i, j, q]
@@ -123,29 +132,111 @@
         return pltpu.make_async_remote_copy(src_ref=src, dst_ref=dst, send_sem=ss, recv_sem=rs,
                                             device_id=(dev,), device_id_type=MESH)
 
-    def span(kind, k):
-        if kind == 2:
-            return (NG - 1) * GR + k * TR, TR
-        return (kind * 8 + k) * GR, GR
-
-    def zslice(ref, kind, k):
-        return ref.at[:, rows(*span(kind, k)), :]
+    def span(kind, k, hb=0):
+        if kind < 2:
+            return (kind * 8 + k) * GR, GR
+        off = sum(PIECES[:k])
+        if off < GR:
+            return (NG - 2) * GR + off, PIECES[k]
+        side = hb if off < GR + SIDE else 1 - hb
+        return (NG - 1) * GR + side * SIDE + off % SIDE, PIECES[k]
 
     def index(kind, k):
-        return k + (0, 8, 15)[kind]
-
-    def own_copy(kind, k):
-        return remote(zslice(psi, kind, k), zslice(bo, kind, k), ps, bor.at[index(kind, k)], dev_mid)
-
-    def up_copy(kind, k):
-        return remote(zslice(psi, kind, k), zslice(abuf, kind, k), ps, ar.at[index(kind, k)], dev_in)
-
-    def fwd_copy(kind, k):
-        return remote(zslice(abuf, kind, k), zslice(bf, kind, k), fs, bfr.at[index(kind, k)], dev_mid)
-
-    def down_copy(kind, k):
-        return remote(zslice(bf, kind, k), zslice(bo, kind, k), os_, bor.at[index(kind, k)], dev_out)
-
+        return k + (0, 8, NG - 2)[kind]
+
+    def zcopy(src, dst, ss, rs, dev, place):
+        return remote(src.at[:, rows(*place), :], dst.at[:, rows(*place), :], ss, rs, dev)
+
+    def own_copy(kind, k, place):
+        return zcopy(psi, bo, ps, br.at[index(kind, k)], dev_mid, place)
+
+    def up_copy(c, place):
+        return zcopy(psi, abuf, ps, ar.at[c], dev_in, place)
+
+    def fwd_copy(kind, k, place):
+        return zcopy(abuf, bf, fs, br.at[index(kind, k)], dev_mid, place)
+
+    def down_copy(kind, k, place):
+        return zcopy(bf, bo, os_, br.at[index(kind, k)], dev_out, place)
+
+    def direct(hb):
+        return NG * GR - hb * SIDE - DR
+
+    early_copy = zcopy(psi, abuf, ps, er, dev_out, (direct(1 - b), DR))
+    dev_far = sub + 24 * (1 - b)
+
+    def part(ref, k):
+        return ref.at[:, pl.ds(k * DP, DP), :]
+
+    def far_copy(k):
+        return remote(part(pf, k), part(rp, k), os_, dr.at[k], dev_far)
+
+    def mid_copy(k):
+        return remote(part(pm, k), part(rp, k), fs, dr.at[k], dev_mid)
+
+    def send_both(kind, k, hb=0):
+        own_copy(kind, k, span(kind, k, hb)).start()
+        fwd_copy(kind, k, span(kind, k, hb)).start()
+
+    g5 = gate(5)
+
+    def gate5(c, slot, start=0, size=GR):
+        def body(i):
+            r = start + i * BLK
+            s0 = (slot * GR + r) * 2
+            s1 = s0 + 2 * GR
+            lo = st[pl.ds(s0, BLK, stride=2), :], st[pl.ds(s0 + 1, BLK, stride=2), :]
+            hi = st[pl.ds(s1, BLK, stride=2), :], st[pl.ds(s1 + 1, BLK, stride=2), :]
+            n0, n1 = apply_pair(g5, lo, hi)
+            store(psi, c * GR + r, BLK, n0)
+            store(psi, (c + 8) * GR + r, BLK, n1)
+        loop(size // BLK, body)
+
+    def send_first(c, start=0, size=GR):
+        place = (c * GR + start, size)
+
+        @pl.when(inner)
+        def _():
+            own_copy(0, c, place).start()
+
+        @pl.when(outer)
+        def _():
+            up_copy(c, place).start()
+
+    for cp in part_a:
+        cp.wait()
+    gate5(0, 0, 0, FIRST)
+
+    @pl.when(inner)
+    def _():
+        pl.semaphore_wait(barrier, 5)
+
+    @pl.when(outer)
+    def _():
+        pl.semaphore_wait(barrier, 4)
+    send_first(0, 0, FIRST)
+    for cp in part_b:
+        cp.wait()
+    for cp in in_pair(1, 2, 2):
+        cp.start()
+    gate5(0, 0, FIRST, GR - FIRST)
+    send_first(0, FIRST, GR - FIRST)
+
+    def phase0(m):
+        c = m + 1
+        slot = 2 * (c % 2)
+        nxt = 2 - slot
+
+        @pl.when(c < 7)
+        def _():
+            for cp in in_pair(c + 1, nxt, nxt):
+                cp.start()
+        for cp in in_pair(c, slot, slot):
+            cp.wait()
+        gate5(c, slot)
+        send_first(c)
+    loop(7, phase0)
+    cz_copy.wait()
     def z_row(hi, lo):
         return [cprod(u(0, hi, v), u(1, lo, w)) for v, w in ((b, 1 - b), (b, b), (1 - b, b), (1 - b, 1 - b))]
     w_own = z_row(b, 1 - b)
@@ -155,25 +246,25 @@
 
     def fold(d):
         t = d[0:8]
-        for j in range(1, BLK // 8):
+        for j in range(1, d.shape[0] // 8):
             t = t + d[8 * j:8 * j + 8]
         return t
 
     def finish_z(kind, k, count=2):
-        start, size = span(kind, k)
+        start, size = span(kind, k, 1 - b)
+        blk = min(BLK, size)
 
         @pl.when(inner)
         def _():
-            own_copy(kind, k).wait_recv()
-            fwd_copy(kind, k).wait_recv()
+            zcopy(psi, bo, ps, br.at[index(kind, k)], dev_mid, (0, 2 * size)).wait_recv()
 
             def body(i):
-                s = start + i * BLK
-                vals = (load(psi, s, BLK), load(abuf, s, BLK), load(bo, s, BLK), load(bf, s, BLK))
+                s = start + i * blk
+                vals = (load(psi, s, blk), load(abuf, s, blk), load(bo, s, blk), load(bf, s, blk))
                 own = cmac(tuple(zip(w_own, vals)))
                 out = cmac(tuple(zip(w_out, vals)))
-                store(bf, s, BLK, out)
-                store(bo, s, BLK, own)
+                store(bf, s, blk, out)
+                store(bo, s, blk, own)
                 if kind and count:
                     d_own = norm2(own)
                     d_out = norm2(out)
@@ -184,16 +275,16 @@
                         d_far = norm2(cmac(tuple(zip(w_far, vals))))
                         d0, d1 = near - (d_mid + d_far), d1 + (d_far - d_mid)
                         near = near + (d_mid + d_far)
-                    acc[rows(s % SR, BLK), :] += near
+                    acc[rows(s % SR, blk), :] += near
                     tot[s // SR] += fold(near)
                     diff[0] += fold(d0)
                     diff[1] += fold(d1)
-            loop(size // BLK, body)
-            down_copy(kind, k).start()
+            loop(size // blk, body)
+            down_copy(kind, k, (start, size)).start()
 
         @pl.when(outer)
         def _():
-            down_copy(kind, k).wait_recv()
+            down_copy(kind, k, (start, size)).wait_recv()
 
     def xchg(state, c, stage):
         buf, ss, rs, dev = ((xb, xs, xr, dev_x), (yb, ys, yr, dev_y), (cb, cs, cr_, dev_c))[stage]
@@ -254,46 +345,6 @@
             for j in range(8):
                 store(state, first_row + j * GR + i * 8, 8, p[j])
         loop(GR // 8, body)
-
-    g5 = gate(5)
-
-    def phase0(c):
-        slot = 2 * (c % 2)
-        nxt = 2 - slot
-
-        @pl.when(c < 7)
-        def _():
-            in_copy(c + 1, nxt).start()
-            in_copy(c + 9, nxt + 1).start()
-        in_copy(c, slot).wait()
-        in_copy(c + 8, slot + 1).wait()
-
-        def body(i):
-            s0 = slot * 2 * GR + i * 2 * BLK
-            s1_ = s0 + 2 * GR
-            lo = st[pl.ds(s0, BLK, stride=2), :], st[pl.ds(s0 + 1, BLK, stride=2), :]
-            hi = st[pl.ds(s1_, BLK, stride=2), :], st[pl.ds(s1_ + 1, BLK, stride=2), :]
-            n0, n1 = apply_pair(g5, lo, hi)
-            store(psi, c * GR + i * BLK, BLK, n0)
-            store(psi, (c + 8) * GR + i * BLK, BLK, n1)
-        loop(GR // BLK, body)
-
-        @pl.when(jnp.logical_and(inner, c == 0))
-        def _():
-            pl.semaphore_wait(barrier, 5)
-
-        @pl.when(jnp.logical_and(outer, c == 0))
-        def _():
-            pl.semaphore_wait(barrier, 4)
-
-        @pl.when(inner)
-        def _():
-            own_copy(0, c).start()
-
-        @pl.when(outer)
-        def _():
-            up_copy(0, c).start()
-    loop(8, phase0)
 
     row = lax.broadcasted_iota(jnp.int32, (128, 128), 0)
     col = lax.broadcasted_iota(jnp.int32, (128, 128), 1)
@@ -328,8 +379,8 @@
 
             @pl.when(inner)
             def _():
-                up_copy(0, i).wait_recv()
-                fwd_copy(0, i).start()
+                up_copy(i, span(0, i)).wait_recv()
+                fwd_copy(0, i, span(0, i)).start()
 
         @pl.when(jnp.logical_and(i >= 1, i < 9))
         def _():
@@ -347,7 +398,7 @@
 
             @pl.when(outer)
             def _():
-                up_copy(1, i - 3).start()
+                up_copy(5 + i, span(1, i - 3)).start()
     loop(11, phase2)
 
     def phase3(i):
@@ -355,20 +406,24 @@
         def _():
             @pl.when(inner)
             def _():
-                @pl.when(i < 7)
+                @pl.when(i < 6)
                 def _():
-                    own_copy(1, i).start()
-                    up_copy(1, i).wait_recv()
-                    fwd_copy(1, i).start()
+                    own_copy(1, i, span(1, i)).start()
+                    up_copy(8 + i, span(1, i)).wait_recv()
+                    fwd_copy(1, i, span(1, i)).start()
+
+                @pl.when(i == 6)
+                def _():
+                    up_copy(8 + i, span(1, i)).wait_recv()
+                    for k in (0, 1):
+                        send_both(2, k, b)
 
                 @pl.when(i == 7)
                 def _():
-                    up_copy(1, 7).wait_recv()
-                    def pieces(t):
-                        p = (t + b * (NT // 2)) % NT
-                        own_copy(2, p).start()
-                        fwd_copy(2, p).start()
-                    loop(NT, pieces)
+                    up_copy(8 + i, span(1, i)).wait_recv()
+                    for k in (2, 3, 4):
+                        send_both(2, k, b)
+                    early_copy.start()
             finish_z(0, i)
             local_gates(bo, i)
             xchg(bo, i, 0).start()
@@ -392,25 +447,29 @@
     flat = lax.broadcasted_iota(jnp.int32, (BLK, LANES), 0) * LANES + lax.broadcasted_iota(jnp.int32, (BLK, LANES), 1)
     shifts = [(NQ - 1 - cz_ref[0, p], NQ - 1 - cz_ref[1, p]) for p in range(12)]
 
+    def put(s, re, im, blk):
+        idx = flat[:blk] + (me * (ROWS * LANES) + s * LANES)
+        par = None
+        for sa, sb in shifts:
+            t = lax.shift_right_logical(idx, sa) & lax.shift_right_logical(idx, sb)
+            par = t if par is None else par ^ t
+        sign = (1 - 2 * (par & 1)).astype(jnp.float32)
+        o_ref[pl.ds(2 * s, blk, stride=2), :] = re * sign
+        o_ref[pl.ds(2 * s + 1, blk, stride=2), :] = im * sign
+
     def emit(kind, k):
-        start, size = span(kind, k)
+        start, size = span(kind, k, 1 - b)
+        blk = min(BLK, size)
 
         def body(i):
-            s = start + i * BLK
-            re, im = load(bo, s, BLK)
-            idx = flat + (me * (ROWS * LANES) + s * LANES)
-            par = None
-            for sa, sb in shifts:
-                t = lax.shift_right_logical(idx, sa) & lax.shift_right_logical(idx, sb)
-                par = t if par is None else par ^ t
-            sign = (1 - 2 * (par & 1)).astype(jnp.float32)
+            s = start + i * blk
+            re, im = load(bo, s, blk)
             if not kind:
                 d = norm2((re, im))
-                acc[rows(s % SR, BLK), :] += d
+                acc[rows(s % SR, blk), :] += d
                 tot[s // SR] += fold(d)
-            o_ref[pl.ds(2 * s, BLK, stride=2), :] = re * sign
-            o_ref[pl.ds(2 * s + 1, BLK, stride=2), :] = im * sign
-        loop(size // BLK, body)
+            put(s, re, im, blk)
+        loop(size // blk, body)
 
     sl = lax.broadcasted_iota(jnp.int32, (8, LANES), 0)
     ln = lax.broadcasted_iota(jnp.int32, (8, LANES), 1)
@@ -450,6 +509,12 @@
 
     @pl.when(inner)
     def _():
+        def partial(i):
+            s = direct(b) + i * BLK
+            vals = load(psi, s, BLK), load(abuf, s, BLK)
+            store(pm, i * BLK, BLK, cmac(tuple(zip(w_mid, vals))))
+            store(pf, i * BLK, BLK, cmac(tuple(zip(w_far, vals))))
+        loop(DR // BLK, partial)
         up_sums.wait_recv()
         fvec[...] += gvec[...]
         acc[...] = jnp.zeros_like(acc)
@@ -458,34 +523,59 @@
     def phase5(k):
         finish_z(1, k)
         emit(1, k)
-    loop(7, phase5)
-
-    def tail(t, count):
-        p = (t + (1 - b) * (NT // 2)) % NT
-        finish_z(2, p, count)
-        emit(2, p)
-    loop(NT // 2, lambda t: tail(t, 4))
+    loop(6, phase5)
+    for k in (0, 1, 2):
+        finish_z(2, k, 4 if k == 2 else 2)
+        emit(2, k)
+    finish_z(2, 3, 4)
 
     mine = b * 8 + sub
 
     def msg_copy(r):
-        return remote(msg.at[mine], msg.at[mine], ms, mr.at[mine], (me + r) % 32)
+        return remote(msg.at[mine], msg.at[mine], ms, mr, (me + r) % 32)
 
     @pl.when(inner)
     def _():
         wide = jnp.concatenate([fvec[...] + sums(1), jnp.zeros((LANES - 32, LANES), jnp.float32)], axis=0)
         msg[pl.ds(mine, 1)] = jnp.sum(wide.T, axis=0, keepdims=True)[None]
         loop(31, lambda r: msg_copy(r + 1).start())
-
-    loop(NT // 2, lambda t: tail(t + NT // 2, 0))
-
-    def receive(t):
-        dev = t % 8 + 8 * (1 + t // 8)
-
-        @pl.when(dev != me)
-        def _():
-            remote(msg.at[t], msg.at[t], ms, mr.at[t], dev).wait_recv()
-    loop(16, receive)
+        for k in (5, 6):
+            send_both(2, k, b)
+        for k in range(DR // DP):
+            far_copy(k).start()
+        for k in range(DR // DP):
+            mid_copy(k).start()
+    emit(2, 3)
+    for k in (4, 5, 6):
+        finish_z(2, k, 0)
+        emit(2, k)
+
+    @pl.when(outer)
+    def _():
+        early_copy.wait_recv()
+    w_near = [tuple(jnp.where(inner, p, q) for p, q in zip(*pair)) for pair in zip(w_own, (w_out[1], w_out[0]))]
+    for k in range(DR // DP):
+        mid_copy(k).wait_recv()
+
+        def add_up(i):
+            t = k * DP + i * BLK
+            s = direct(1 - b) + t
+            re, im = cmac(tuple(zip(w_near, (load(psi, s, BLK), load(abuf, s, BLK)))))
+            far = load(rp, t, BLK)
+            put(s, re + far[0], im + far[1], BLK)
+        loop(DP // BLK, add_up)
+
+    def receive(count):
+        got = msg.at[pl.ds(0, count)]
+        remote(got, got, ms, mr, dev_mid).wait_recv()
+
+    @pl.when(inner)
+    def _():
+        receive(15)
+
+    @pl.when(outer)
+    def _():
+        receive(16)
     val = msg[0]
     for t in range(1, 16):
         val = val + msg[t]
@@ -540,10 +630,13 @@
                 pltpu.VMEM((32, LANES), jnp.float32),
                 pltpu.VMEM((16, 1, LANES), jnp.float32),
                 pltpu.VMEM((31, 1, LANES), jnp.float32),
+                pltpu.VMEM((2, DR, LANES), jnp.float32),
+                pltpu.VMEM((2, DR, LANES), jnp.float32),
+                pltpu.VMEM((2, DR, LANES), jnp.float32),
                 pltpu.SMEM((2, 2, 2, NQ), jnp.float32),
                 pltpu.SMEM((2, 12), jnp.int32),
-                dma((2,)), dma((4,)), dma(()), dma((16,)), dma((15 + NT,)), dma((15 + NT,)), dma(()), dma(())] + [
-                dma((2,)), dma((NX,))] * 3 + [dma(()), dma(()), dma(()), dma((16,))],
+                dma((2,)), dma((4,)), dma(()), dma((NG,)), dma((NZ,)), dma(()), dma(())] + [
+                dma((2,)), dma((NX,))] * 3 + [dma(())] * 5 + [dma((DR // DP,))],
             compiler_params=pltpu.CompilerParams(has_side_effects=True, collective_id=0,
                                                  vmem_limit_bytes=VMEM_LIMIT),
         )(x, gates, cz_pairs.transpose(1, 0))

time: 374 us -> 370 us (0.989)
  Pallas kernels: 373 us -> 369 us
    pallas_call x1, Pallas kernels: 370 us -> 366 us  [local_layer(): pl.pallas_call(kernel, name='gate_layer', out_shape=(pltpu.VMEM((2 * ROWS...]
where the time goes in v5:
time: 370 us
  Pallas kernels  369 us (100%)
    pallas_call x1, Pallas kernels, local_layer(): pl.pallas_call(kernel, name='gate_layer', out_shape=(pltpu.VMEM((2 * ROWS...  366 us

profile of v5, /device:TPU:0, one launch (start us, length us, event | category | flops | bytes accessed | tf_op | source)
XLA Modules:
  0.0 369.9 jit_solution(13639989702020022307)
XLA Ops:
  0.6 365.8 %gate_layer.1 = (f32[16384,128]{1,0:T(8,128)S(1)}, f32[1,25]{1,0:T(1,128)S(1)}) custom-call(f32[16384,128]{1,0:T(8,128)} %bitcast.13, f32[2,2,2,25]{3,2,1,0:T(2,128)} %bitcast.14, s32[2,12]{1,0:T(2,128)} %bitcast.15), custom_call_target="tpu_custom_call" | custom-call | tf_op jit(solution)/shard_map/gate_layer/pallas_call | solution.py:614
  366.5 3.4 write_result.1

commit v6 on v5

--- a/solution.py
+++ b/solution.py
@@ -10,10 +10,10 @@
 ROWS = 8192
 NG = 16
 GR = ROWS // NG
-PIECES = (256, 256, 128, 128, 64, 32, 32)
-SIDE = GR // 2
-DR = 128
+PIECES = (256, 128, 64, 64)
+DR = GR
 DP = 64
+ND = DR // DP
 NT = len(PIECES)
 NZ = NG - 2 + NT
 FIRST = 128
@@ -135,11 +135,7 @@
     def span(kind, k, hb=0):
         if kind < 2:
             return (kind * 8 + k) * GR, GR
-        off = sum(PIECES[:k])
-        if off < GR:
-            return (NG - 2) * GR + off, PIECES[k]
-        side = hb if off < GR + SIDE else 1 - hb
-        return (NG - 1) * GR + side * SIDE + off % SIDE, PIECES[k]
+        return (NG - 2 + hb) * GR + sum(PIECES[:k]), PIECES[k]
 
     def index(kind, k):
         return k + (0, 8, NG - 2)[kind]
@@ -160,13 +156,13 @@
         return zcopy(bf, bo, os_, br.at[index(kind, k)], dev_out, place)
 
     def direct(hb):
-        return NG * GR - hb * SIDE - DR
+        return (NG - 1 - hb) * GR
 
     early_copy = zcopy(psi, abuf, ps, er, dev_out, (direct(1 - b), DR))
     dev_far = sub + 24 * (1 - b)
 
     def part(ref, k):
-        return ref.at[:, pl.ds(k * DP, DP), :]
+        return ref.at[:, rows(k * DP, DP), :]
 
     def far_copy(k):
         return remote(part(pf, k), part(rp, k), os_, dr.at[k], dev_far)
@@ -412,17 +408,21 @@
                     up_copy(8 + i, span(1, i)).wait_recv()
                     fwd_copy(1, i, span(1, i)).start()
 
-                @pl.when(i == 6)
-                def _():
-                    up_copy(8 + i, span(1, i)).wait_recv()
-                    for k in (0, 1):
-                        send_both(2, k, b)
-
                 @pl.when(i == 7)
                 def _():
-                    up_copy(8 + i, span(1, i)).wait_recv()
-                    for k in (2, 3, 4):
+                    for k in (6, 7):
+                        up_copy(8 + k, span(1, k)).wait_recv()
+
+                    def partial(j):
+                        s = direct(b) + j * BLK
+                        vals = load(psi, s, BLK), load(abuf, s, BLK)
+                        store(pm, j * BLK, BLK, cmac(tuple(zip(w_mid, vals))))
+                        store(pf, j * BLK, BLK, cmac(tuple(zip(w_far, vals))))
+                    loop(DR // BLK, partial)
+                    loop(ND, lambda k: far_copy(k).start())
+                    for k in range(NT):
                         send_both(2, k, b)
+                    mid_copy(0).start()
                     early_copy.start()
             finish_z(0, i)
             local_gates(bo, i)
@@ -509,12 +509,6 @@
 
     @pl.when(inner)
     def _():
-        def partial(i):
-            s = direct(b) + i * BLK
-            vals = load(psi, s, BLK), load(abuf, s, BLK)
-            store(pm, i * BLK, BLK, cmac(tuple(zip(w_mid, vals))))
-            store(pf, i * BLK, BLK, cmac(tuple(zip(w_far, vals))))
-        loop(DR // BLK, partial)
         up_sums.wait_recv()
         fvec[...] += gvec[...]
         acc[...] = jnp.zeros_like(acc)
@@ -524,10 +518,10 @@
         finish_z(1, k)
         emit(1, k)
     loop(6, phase5)
-    for k in (0, 1, 2):
-        finish_z(2, k, 4 if k == 2 else 2)
+    for k in range(NT - 1):
+        finish_z(2, k, 4)
         emit(2, k)
-    finish_z(2, 3, 4)
+    finish_z(2, NT - 1, 4)
 
     mine = b * 8 + sub
 
@@ -539,22 +533,15 @@
         wide = jnp.concatenate([fvec[...] + sums(1), jnp.zeros((LANES - 32, LANES), jnp.float32)], axis=0)
         msg[pl.ds(mine, 1)] = jnp.sum(wide.T, axis=0, keepdims=True)[None]
         loop(31, lambda r: msg_copy(r + 1).start())
-        for k in (5, 6):
-            send_both(2, k, b)
-        for k in range(DR // DP):
-            far_copy(k).start()
-        for k in range(DR // DP):
-            mid_copy(k).start()
-    emit(2, 3)
-    for k in (4, 5, 6):
-        finish_z(2, k, 0)
-        emit(2, k)
+        loop(ND - 1, lambda k: mid_copy(k + 1).start())
+    emit(2, NT - 1)
 
     @pl.when(outer)
     def _():
         early_copy.wait_recv()
     w_near = [tuple(jnp.where(inner, p, q) for p, q in zip(*pair)) for pair in zip(w_own, (w_out[1], w_out[0]))]
-    for k in range(DR // DP):
+
+    def take(k):
         mid_copy(k).wait_recv()
 
         def add_up(i):
@@ -564,6 +551,7 @@
             far = load(rp, t, BLK)
             put(s, re + far[0], im + far[1], BLK)
         loop(DP // BLK, add_up)
+    loop(ND, take)
 
     def receive(count):
         got = msg.at[pl.ds(0, count)]
@@ -636,7 +624,7 @@
                 pltpu.SMEM((2, 2, 2, NQ), jnp.float32),
                 pltpu.SMEM((2, 12), jnp.int32),
                 dma((2,)), dma((4,)), dma(()), dma((NG,)), dma((NZ,)), dma(()), dma(())] + [
-                dma((2,)), dma((NX,))] * 3 + [dma(())] * 5 + [dma((DR // DP,))],
+                dma((2,)), dma((NX,))] * 3 + [dma(())] * 5 + [dma((ND,))],
             compiler_params=pltpu.CompilerParams(has_side_effects=True, collective_id=0,
                                                  vmem_limit_bytes=VMEM_LIMIT),
         )(x, gates, cz_pairs.transpose(1, 0))

time: 370 us -> 369 us (level)
  no operation moved by 1% of the time
where the time goes in v6:
time: 369 us; the launch traced here: 367 us
  Pallas kernels  366 us (99%)
    pallas_call x1, Pallas kernels, local_layer(): pl.pallas_call(kernel, name='gate_layer', out_shape=(pltpu.VMEM((2 * ROWS...  363 us

profile of v6, /device:TPU:0, one launch (start us, length us, event | category | flops | bytes accessed | tf_op | source)
XLA Modules:
  0.0 366.8 jit_solution(14375134231341195447)
XLA Ops:
  0.6 362.7 %gate_layer.1 = (f32[16384,128]{1,0:T(8,128)S(1)}, f32[1,25]{1,0:T(1,128)S(1)}) custom-call(f32[16384,128]{1,0:T(8,128)} %bitcast.13, f32[2,2,2,25]{3,2,1,0:T(2,128)} %bitcast.14, s32[2,12]{1,0:T(2,128)} %bitcast.15), custom_call_target="tpu_custom_call" | custom-call | tf_op jit(solution)/shard_map/gate_layer/pallas_call | solution.py:602
  363.4 3.4 write_result.1

commit v7 on v6

--- a/solution.py
+++ b/solution.py
@@ -16,7 +16,7 @@
 ND = DR // DP
 NT = len(PIECES)
 NZ = NG - 2 + NT
-FIRST = 128
+FIRST = 64
 SR = 128
 NS = 32
 HALF = ROWS // 2
@@ -90,14 +90,13 @@
     def greet(dev):
         pl.semaphore_signal(barrier, inc=1, device_id=(dev,), device_id_type=MESH)
 
+    @pl.when(inner)
+    def _():
+        greet(dev_mid)
+        greet(dev_out)
+    greet(dev_y)
     greet(dev_x)
-    greet(dev_y)
     greet(dev_c)
-    greet(dev_mid)
-
-    @pl.when(inner)
-    def _():
-        greet(dev_out)
     u_copy = pltpu.make_async_copy(u_hbm, u_ref, par_sem.at[0])
     cz_copy = pltpu.make_async_copy(cz_hbm, cz_ref, par_sem.at[1])
     u_copy.start()
@@ -203,13 +202,7 @@
         cp.wait()
     gate5(0, 0, 0, FIRST)
 
-    @pl.when(inner)
-    def _():
-        pl.semaphore_wait(barrier, 5)
-
-    @pl.when(outer)
-    def _():
-        pl.semaphore_wait(barrier, 4)
+    pl.semaphore_wait(barrier, 4)
     send_first(0, 0, FIRST)
     for cp in part_b:
         cp.wait()

time: 369 us -> 369 us (level)
  no operation moved by 1% of the time
where the time goes in v7:
time: 369 us; the launch traced here: 367 us
  Pallas kernels  366 us (99%)
    pallas_call x1, Pallas kernels, local_layer(): pl.pallas_call(kernel, name='gate_layer', out_shape=(pltpu.VMEM((2 * ROWS...  363 us

profile of v7, /device:TPU:0, one launch (start us, length us, event | category | flops | bytes accessed | tf_op | source)
XLA Modules:
  0.0 366.8 jit_solution(6508295163032982526)
XLA Ops:
  0.6 362.8 %gate_layer.1 = (f32[16384,128]{1,0:T(8,128)S(1)}, f32[1,25]{1,0:T(1,128)S(1)}) custom-call(f32[16384,128]{1,0:T(8,128)} %bitcast.13, f32[2,2,2,25]{3,2,1,0:T(2,128)} %bitcast.14, s32[2,12]{1,0:T(2,128)} %bitcast.15), custom_call_target="tpu_custom_call" | custom-call | tf_op jit(solution)/shard_map/gate_layer/pallas_call | solution.py:595
  363.4 3.4 write_result.1
